TPU v7x, 32 devices: a whole 2x2x4 slice. The times are simulated.
32 devices in a mesh: dp: 8 (over y, x, core), tensor: 4 (over z).
Axes of the slice: x: 2, y: 2, z: 4, core: 2. Of those that a mesh axis runs over, the one named last changes fastest.
Arguments:
- hidden_states: float32 [4096, 2048], P(('dp', 'tensor')), may hold values from -40 to 40
- lengths: int32 [8], P('dp'), may hold values from 128 to 512
- shard_order: int32 [8], replicated, may hold values from 0 to 7, each once
- gain_attn: float32 [2048], replicated, may hold values from 0.25 to 1.75
- w_query: bfloat16 [2048, 2048], P('dp', 'tensor'), may hold values from -0.015625 to 0.015625
- w_key: bfloat16 [2048, 2048], P('dp', 'tensor'), may hold values from -0.125 to 0.125
- w_value: bfloat16 [2048, 2048], P('dp', 'tensor'), may hold values from -0.125 to 0.125
- w_out: bfloat16 [2048, 2048], P('tensor', 'dp'), may hold values from -1 to 1
- rel_bias: float32 [32, 32], P(None, 'tensor'), may hold values from -6 to 300
- gain_ff: float32 [2048], replicated, may hold values from 0.25 to 1.75
- w_gate: bfloat16 [2048, 5120], P('dp', 'tensor'), may hold values from -0.125 to 0.125
- w_up: bfloat16 [2048, 5120], P('dp', 'tensor'), may hold values from -0.125 to 0.125
- w_down: bfloat16 [5120, 2048], P('tensor', 'dp'), may hold values from -0.078125 to 0.078125
- gain_final: float32 [2048], replicated, may hold values from 0.25 to 1.75
- w_reward: float32 [2048], replicated, may hold values from -0.125 to 0.125
Outputs:
- layer_output: float32 [4096, 2048], P(('dp', 'tensor'))
- normalized_rewards: float32 [8], P('dp')
Inputs may be any that keep to these rules, and one draw needn't show every extreme that they name: `shard_order`: each of 0 to 8 - 1 appears once. `lengths`: positions at or beyond a rollout's length are padding.
All inputs are finite; a program needn't handle non-finite values.
Results may differ from a plain program's by a relative error of at most 0.02.
Values may be sent and summed in bfloat16 or wider, within the bound.
No kernel may reach another device: no remote copies, remote signals or barrier semaphores. Data moves between devices by JAX's collectives and lax.ppermute only.
A program may use at most 128 MiB of HBM per device.

v0:
```python
import functools

import jax
import jax.numpy as jnp
from jax import lax
from jax.experimental import pallas as pl
from jax.experimental.pallas import tpu as pltpu
from jax.sharding import PartitionSpec as P


DK = 64
TILE = 128

bucket_edges = (12, 16, 23, 32, 46, 64, 91)


def bucket_index(relative):
    distance = jnp.abs(relative)
    bucket_low = jnp.minimum(distance, 8)
    for threshold in bucket_edges:
        bucket_low = bucket_low + (distance >= threshold).astype(jnp.int32)
    return jnp.where(relative > 0, 16, 0) + bucket_low


def rms_norm(values_in, weight_gain):
    return (
        values_in
        * lax.rsqrt(jnp.mean(values_in * values_in, axis=-1, keepdims=True) + 1e-06)
        * weight_gain
    )


def reorder_blocks(values_in, ordering):
    full_shape = values_in.shape
    blocks = values_in.reshape(
        full_shape[:-1] + (ordering.shape[0], full_shape[-1] // ordering.shape[0])
    )
    return jnp.take(blocks, ordering, axis=-2).reshape(full_shape)


def ring_pairs(step):
    size = lax.axis_size("tensor")
    return [(i, (i + step) % size) for i in range(size)]


def ring_gather(block):
    size = lax.axis_size("tensor")
    if size != 4:
        return lax.all_gather(block, "tensor", axis=0, tiled=True)
    rows = block.shape[0]
    half = rows // 2
    here = lax.axis_index("tensor")
    before = lax.ppermute(block, "tensor", ring_pairs(1))
    after = lax.ppermute(block, "tensor", ring_pairs(-1))
    far_low = lax.ppermute(before[:half], "tensor", ring_pairs(1))
    far_high = lax.ppermute(after[half:], "tensor", ring_pairs(-1))
    whole = jnp.zeros((size * rows,) + block.shape[1:], block.dtype)
    zero = jnp.int32(0)
    for piece, shift, offset in (
        (block, 0, 0),
        (before, 3, 0),
        (after, 1, 0),
        (far_low, 2, 0),
        (far_high, 2, half),
    ):
        start = ((here + shift) % size) * rows + offset
        whole = lax.dynamic_update_slice(whole, piece, (start, zero))
    return whole


def ring_scatter(partial):
    size = lax.axis_size("tensor")
    if size != 4:
        return lax.psum_scatter(partial, "tensor", scatter_dimension=0, tiled=True).astype(
            jnp.float32
        )
    rows = partial.shape[0] // size
    half = rows // 2
    here = lax.axis_index("tensor")

    def rows_of(shift):
        start = ((here + shift) % size) * rows
        return lax.dynamic_slice(partial, (start, jnp.int32(0)), (rows, partial.shape[1]))

    far = rows_of(2)
    low = lax.ppermute(far[:half], "tensor", ring_pairs(1))
    high = lax.ppermute(far[half:], "tensor", ring_pairs(-1))
    ahead = rows_of(1)
    behind = rows_of(3)
    ahead = jnp.concatenate(
        [
            (ahead[:half].astype(jnp.float32) + low.astype(jnp.float32)).astype(partial.dtype),
            ahead[half:],
        ]
    )
    behind = jnp.concatenate(
        [
            behind[:half],
            (behind[half:].astype(jnp.float32) + high.astype(jnp.float32)).astype(partial.dtype),
        ]
    )
    from_before = lax.ppermute(ahead, "tensor", ring_pairs(1))
    from_after = lax.ppermute(behind, "tensor", ring_pairs(-1))
    return (
        rows_of(0).astype(jnp.float32)
        + from_before.astype(jnp.float32)
        + from_after.astype(jnp.float32)
    )


def attention_kernel(length_ref, q_ref, k_ref, v_ref, bias_ref, o_ref):
    span = q_ref.shape[0]
    lanes = q_ref.shape[1]
    blocks = span // TILE
    length = length_ref[0]
    keys = k_ref[...]
    values = v_ref[...]
    valid = lax.broadcasted_iota(jnp.int32, (1, span), 1) < length
    first_head = lax.broadcasted_iota(jnp.int32, (1, lanes), 1) < DK
    contexts = []
    for head in range(2):
        table = bias_ref[0, head : head + 1, :]
        near = pltpu.roll(
            jnp.broadcast_to(table, (TILE, 4 * TILE)), 0, 1, stride=1, stride_axis=0
        )
        own = first_head if head == 0 else jnp.logical_not(first_head)
        far_left = jnp.broadcast_to(table[:, 1:2], (TILE, TILE))
        far_right = jnp.broadcast_to(table[:, 4 * TILE - 1 :], (TILE, TILE))
        pieces = []
        for block in range(blocks):
            queries = q_ref[block * TILE : (block + 1) * TILE, :]
            queries = jnp.where(own, queries, jnp.zeros_like(queries))
            scores = lax.dot_general(
                queries, keys, (((1,), (1,)), ((), ())), preferred_element_type=jnp.float32
            )
            bias = []
            for other in range(blocks):
                delta = other - block
                if delta < -1:
                    bias.append(far_left)
                elif delta > 1:
                    bias.append(far_right)
                else:
                    bias.append(near[:, (delta + 2) * TILE : (delta + 3) * TILE])
            scores = jnp.where(valid, scores + jnp.concatenate(bias, axis=1), -1e30)
            top = jnp.max(scores, axis=-1, keepdims=True)
            weights = jnp.exp(scores - top)
            total = jnp.sum(weights, axis=-1, keepdims=True)
            soft = (weights / total).astype(jnp.bfloat16)
            pieces.append(jnp.dot(soft, values, preferred_element_type=jnp.float32))
        contexts.append(pieces)
    for block in range(blocks):
        o_ref[block * TILE : (block + 1) * TILE, :] = jnp.where(
            first_head, contexts[0][block], contexts[1][block]
        ).astype(o_ref.dtype)


def attention(length, projected, bias_table):
    span, width = projected.shape
    inner = width // 3
    pairs = inner // (2 * DK)
    return pl.pallas_call(
        attention_kernel,
        out_shape=jax.ShapeDtypeStruct((span, inner), jnp.bfloat16),
        grid_spec=pltpu.PrefetchScalarGridSpec(
            num_scalar_prefetch=1,
            grid=(pairs,),
            in_specs=[
                pl.BlockSpec((span, 2 * DK), lambda p, n: (0, p)),
                pl.BlockSpec((span, 2 * DK), lambda p, n: (0, pairs + p)),
                pl.BlockSpec((span, 2 * DK), lambda p, n: (0, 2 * pairs + p)),
                pl.BlockSpec((1, 2, 4 * TILE), lambda p, n: (p, 0, 0)),
            ],
            out_specs=pl.BlockSpec((span, 2 * DK), lambda p, n: (0, p)),
        ),
        cost_estimate=pl.CostEstimate(
            flops=16 * span * span * inner,
            bytes_accessed=2 * span * (width + inner),
            transcendentals=span * span * inner // DK,
        ),
        name="attention",
    )(length, projected, projected, projected, bias_table)


def total_over(values_in, name):
    size = lax.axis_size(name)
    if size > 8:
        return lax.psum(values_in, name)
    total = values_in
    for step in range(1, size):
        total = total + lax.ppermute(
            values_in, name, [(i, (i + step) % size) for i in range(size)]
        )
    return total


def local_general(
    hidden_states,
    lengths,
    shard_order,
    gain_attn,
    w_query,
    w_key,
    w_value,
    w_out,
    rel_bias,
    gain_ff,
    w_gate,
    w_up,
    w_down,
    gain_final,
    w_reward,
):
    groups = shard_order.shape[0]
    block_ids = jnp.arange(groups, dtype=jnp.int32)
    inverse = jnp.sum(
        block_ids[:, None] * (shard_order[:, None] == block_ids[None, :]).astype(jnp.int32), axis=0
    )
    own_rows = reorder_blocks(hidden_states, shard_order)
    attn_gain = reorder_blocks(gain_attn, shard_order)
    feed_gain = reorder_blocks(gain_ff, shard_order)
    final_gain = reorder_blocks(gain_final, shard_order)
    reward_head = reorder_blocks(w_reward, shard_order)
    row_count = own_rows.shape[0]
    row_start = lax.axis_index("tensor") * row_count

    qkv_full = lax.all_gather(
        jnp.concatenate([w_query, w_key, w_value], axis=1), "dp", axis=0, tiled=True
    )
    out_full = lax.all_gather(w_out, "dp", axis=1, tiled=True)
    gate_up_full = lax.all_gather(
        jnp.concatenate([w_gate, w_up], axis=1), "dp", axis=0, tiled=True
    )
    down_full = lax.all_gather(w_down, "dp", axis=1, tiled=True)

    normed = ring_gather(rms_norm(own_rows, attn_gain).astype(jnp.bfloat16))
    projected = jnp.dot(normed, qkv_full, preferred_element_type=jnp.float32).astype(jnp.bfloat16)

    heads = rel_bias.shape[1]
    relative = jnp.arange(4 * TILE, dtype=jnp.int32) - 2 * TILE
    onehot = (
        bucket_index(relative)[:, None]
        == jnp.arange(rel_bias.shape[0], dtype=jnp.int32)[None, :]
    ).astype(jnp.float32)
    bias_table = jnp.dot(onehot, rel_bias, precision=lax.Precision.HIGHEST).T
    bias_table = bias_table.reshape(heads // 2, 2, 4 * TILE)
    length = lengths[0]
    context = attention(lengths, projected, bias_table)

    attn_partial = jnp.dot(context, out_full, preferred_element_type=jnp.float32).astype(
        jnp.bfloat16
    )
    mid_own = own_rows + ring_scatter(attn_partial)
    mid_normed = ring_gather(rms_norm(mid_own, feed_gain).astype(jnp.bfloat16))
    hidden_width = w_gate.shape[1]
    gate_up = jnp.dot(mid_normed, gate_up_full, preferred_element_type=jnp.float32)
    activated = (
        jax.nn.gelu(gate_up[:, :hidden_width], approximate=True) * gate_up[:, hidden_width:]
    ).astype(jnp.bfloat16)
    feed_partial = jnp.dot(activated, down_full, preferred_element_type=jnp.float32).astype(
        jnp.bfloat16
    )
    output_rows = mid_own + ring_scatter(feed_partial)
    final_normed = rms_norm(output_rows, final_gain)
    token_score = jnp.dot(final_normed, reward_head, precision=lax.Precision.HIGHEST)
    positions = row_start + jnp.arange(row_count, dtype=jnp.int32)
    local_pool = jnp.sum(jnp.where(positions < length, token_score, 0.0))
    pooled_sum = total_over(jnp.reshape(local_pool, (1,)), "tensor")
    reward = pooled_sum / length.astype(jnp.float32)
    rollouts = lax.axis_size("dp") * lengths.shape[0]
    moments = total_over(jnp.concatenate([reward, reward * reward]), "dp")
    reward_mean = moments[0] / rollouts
    reward_var = moments[1] / rollouts - reward_mean * reward_mean
    normalized = (reward - reward_mean) / jnp.sqrt(reward_var + 1e-06)
    return (reorder_blocks(output_rows, inverse), normalized)


def put(ref, rows, value):
    ref[pl.ds(pl.multiple_of(rows, TILE // 2), value.shape[0]), :] = value


def slot_row(ids, shift, rows):
    return lax.rem(ids[1] + shift, 4) * rows


def true_block(order, ids, mask):
    return order[lax.bitwise_xor(ids[0], jnp.int32(mask))]


PARTS = ((0, 0), (1, 0), (2, 0), (3, 0), (4, 0), (5, 0), (6, 0), (6, 1), (7, 0), (7, 1))


def placed_rows(order, ids, blocks, block):
    for ref, (mask, part) in zip(blocks, PARTS):
        start = true_block(order, ids, mask) * block + part * (block // 2)
        yield ref, pl.multiple_of(start, block // 2)


def rms_kernel(x_ref, gain_ref, low_ref, high_ref):
    x = x_ref[...]
    scale = lax.rsqrt(jnp.mean(x * x, axis=-1, keepdims=True) + 1e-06)
    normed = (x * scale * gain_ref[...]).astype(jnp.bfloat16)
    half = low_ref.shape[0]
    low_ref[...] = normed[:half]
    high_ref[...] = normed[half:]


def pack_kernel(*refs):
    *sources, out = refs
    rows, at = out.shape[0], 0
    step = 2 * TILE
    wide = [s for s in sources if s.shape[0] == rows]
    tall = [s for s in sources if s.shape[0] != rows]
    if tall:
        for j in range(wide[0].shape[1] // step):
            for s in wide:
                out[:, at : at + step] = s[:, j * step : (j + 1) * step]
                at += step
        for s in tall:
            for j in range(s.shape[0] // rows):
                out[:, at : at + s.shape[1]] = s[j * rows : (j + 1) * rows, :]
                at += s.shape[1]
    else:
        for s in wide:
            out[:, at : at + s.shape[1]] = s[...]
            at += s.shape[1]


def project_kernel(order, ids, *refs):
    pieces = refs[:8]
    blocks = refs[8:18]
    out, x_all, w_all, sems = refs[18:]
    tiles, depth, wide = w_all.shape
    for j in range(tiles):
        for ref, start in placed_rows(order, ids, blocks, depth // 8):
            pltpu.make_async_copy(
                ref.at[:, pl.ds(j * wide, wide)],
                w_all.at[j, pl.ds(start, ref.shape[0]), :],
                sems.at[j],
            ).start()
    rows = pieces[0].shape[0]
    for slot, shift in enumerate((0, 3, 1, 2)):
        base = slot_row(ids, shift, 2 * rows)
        put(x_all, base, pieces[2 * slot][...])
        put(x_all, base + rows, pieces[2 * slot + 1][...])

    @pl.loop(0, tiles)
    def _(j):
        pltpu.make_async_copy(w_all.at[j], w_all.at[j], sems.at[j]).wait()
        out[:, pl.ds(pl.multiple_of(j * wide, wide), wide)] = jnp.dot(
            x_all[...], w_all[j], preferred_element_type=jnp.float32
        ).astype(out.dtype)


def out_kernel(order, ids, context, *refs):
    blocks = refs[:8]
    far_low, far_high, ahead_low, ahead_high, behind_low, behind_high, own = refs[8:15]
    x_all, w_all, sems = refs[15:]
    for mask in range(8):
        where_to = true_block(order, ids, mask)
        pltpu.make_async_copy(blocks[mask], w_all.at[where_to], sems.at[where_to]).start()
    rows = own.shape[0]
    half = rows // 2
    for slot, shift in enumerate((2, 1, 3, 0)):
        start = pl.multiple_of(slot_row(ids, shift, rows), rows)
        x_all[slot * rows : (slot + 1) * rows, :] = context[pl.ds(start, rows), :]
    wide = w_all.shape[2]

    @pl.loop(0, 8)
    def _(n):
        pltpu.make_async_copy(w_all.at[n], w_all.at[n], sems.at[n]).wait()
        columns = pl.ds(pl.multiple_of(n * wide, wide), wide)
        part = jnp.dot(x_all[...], w_all[n], preferred_element_type=jnp.float32).astype(own.dtype)
        for k, ref in enumerate(
            (far_low, far_high, ahead_low, ahead_high, behind_low, behind_high)
        ):
            ref[:, columns] = part[k * half : (k + 1) * half, :]
        own[:, columns] = part[3 * rows :, :]


def gelu(v):
    return 0.5 * v * (1.0 + jnp.tanh(0.7978845608028654 * (v + 0.044715 * (v * v * v))))


def feed_kernel(count, order, ids, *refs):
    pieces = refs[:count]
    blocks = refs[count : count + 10]
    outs = refs[count + 10 : 2 * count + 10]
    x_all, hidden, first, second, sem_first, sem_second = refs[2 * count + 10 :]
    tiles, depth, wide = first.shape
    block = depth // 8
    unit = wide // 2
    for j in range(tiles):
        for ref, start in placed_rows(order, ids, blocks, block):
            pltpu.make_async_copy(
                ref.at[:, pl.ds(j * wide, wide)],
                first.at[j, pl.ds(start, ref.shape[0]), :],
                sem_first.at[j],
            ).start()
    for ref, (mask, part) in zip(blocks, PARTS):
        where_to = true_block(order, ids, mask)
        for j in range(second.shape[1] // block):
            pltpu.make_async_copy(
                ref.at[:, pl.ds(tiles * wide + j * block, block)],
                second.at[
                    where_to, pl.ds(j * block + part * (block // 2), ref.shape[0]), :
                ],
                sem_second.at[where_to],
            ).start()
    rows = pieces[0].shape[0]
    for k in range(count):
        x_all[k * rows : (k + 1) * rows, :] = pieces[k][...]

    @pl.loop(0, tiles)
    def _(j):
        pltpu.make_async_copy(first.at[j], first.at[j], sem_first.at[j]).wait()
        both = jnp.dot(x_all[...], first[j], preferred_element_type=jnp.float32)
        hidden[:, pl.ds(pl.multiple_of(j * unit, unit), unit)] = (
            gelu(both[:, :unit]) * both[:, unit:]
        ).astype(hidden.dtype)

    @pl.loop(0, 8)
    def _(n):
        pltpu.make_async_copy(second.at[n], second.at[n], sem_second.at[n]).wait()
        columns = pl.ds(pl.multiple_of(n * block, block), block)
        part = jnp.dot(hidden[...], second[n], preferred_element_type=jnp.float32).astype(
            outs[0].dtype
        )
        for k in range(count):
            outs[k][:, columns] = part[k * rows : (k + 1) * rows, :]


def residual(base, shares, half):
    own, before_low, before_high, after_low, after_high = shares
    low = base[:half] + (
        own[:half].astype(jnp.float32)
        + before_low[...].astype(jnp.float32)
        + after_low[...].astype(jnp.float32)
    )
    high = base[half:] + (
        own[half:].astype(jnp.float32)
        + before_high[...].astype(jnp.float32)
        + after_high[...].astype(jnp.float32)
    )
    return low, high


def mid_kernel(x_ref, *refs):
    shares, gain_ref, mid_ref, low_ref, high_ref = refs[:5], *refs[5:]
    half = low_ref.shape[0]
    for k, part in enumerate(residual(x_ref, shares, half)):
        mid_ref[k * half : (k + 1) * half, :] = part
        scale = lax.rsqrt(jnp.mean(part * part, axis=-1, keepdims=True) + 1e-06)
        (low_ref, high_ref)[k][...] = (part * scale * gain_ref[...]).astype(jnp.bfloat16)


def final_kernel(length, ids, x_ref, *refs):
    shares, gain_ref, head_ref, out_ref, pool_ref = refs[:5], *refs[5:]
    half = out_ref.shape[0] // 2
    pooled = jnp.zeros((1, 1), jnp.float32)
    for k, part in enumerate(residual(x_ref, shares, half)):
        out_ref[k * half : (k + 1) * half, :] = part
        scale = lax.rsqrt(jnp.mean(part * part, axis=-1, keepdims=True) + 1e-06)
        score = jnp.sum(part * scale * gain_ref[...] * head_ref[...], axis=-1, keepdims=True)
        position = (
            lax.broadcasted_iota(jnp.int32, (half, 1), 0) + ids[1] * (2 * half) + k * half
        )
        pooled = pooled + jnp.sum(
            jnp.where(position < length[0], score, 0.0), axis=0, keepdims=True
        )
    pool_ref[...] = jnp.broadcast_to(pooled, pool_ref.shape)


def whole(array):
    return pl.BlockSpec(array.shape, lambda *_: (0,) * len(array.shape))


def call(kernel, scalars, arrays, raw, outs, scratch, flops, moved):
    single = not isinstance(outs, (list, tuple))
    out_list = [outs] if single else list(outs)
    result = pl.pallas_call(
      kernel,
      out_shape=out_list,
      grid_spec=pltpu.PrefetchScalarGridSpec(
          num_scalar_prefetch=len(scalars),
          grid=(1,),
          in_specs=[whole(a) for a in arrays]
          + [pl.BlockSpec(memory_space=pl.ANY) for _ in raw],
          out_specs=[whole(o) for o in out_list],
          scratch_shapes=scratch,
      ),
      cost_estimate=pl.CostEstimate(flops=flops, bytes_accessed=moved, transcendentals=0),
    )(*scalars, *arrays, *raw)
    return result[0] if single else result


def shift_rows(block, step):
    return lax.ppermute(block, "tensor", ring_pairs(step))


def exchange(block, mask):
    return lax.ppermute(block, "dp", [(i, i ^ mask) for i in range(8)])


def plane_gather(block):
    held = {0: block}
    for mask in (2, 4, 6, 1):
        held[mask] = exchange(block, mask)
    for mask in (3, 5, 7):
        held[mask] = exchange(held[mask ^ 1], 1)
    return [held[mask] for mask in range(8)]


def plane_gather_split(block):
    half = block.shape[0] // 2
    held = {0: block}
    for mask in (2, 4, 1):
        held[mask] = exchange(block, mask)
    low = exchange(held[4][:half], 2)
    high = exchange(held[2][half:], 4)
    for mask in (3, 5):
        held[mask] = exchange(held[mask ^ 1], 1)
    pairs = [exchange(low, 1), exchange(high, 1)]
    return [held[mask] for mask in range(6)] + [low, high] + pairs


def half_gather(low, high):
    before_low = shift_rows(low, 1)
    after_high = shift_rows(high, -1)
    before_high = shift_rows(high, 1)
    after_low = shift_rows(low, -1)
    far_low = shift_rows(before_low, 1)
    far_high = shift_rows(after_high, -1)
    return [low, high, before_low, before_high, after_low, after_high, far_low, far_high]


def add_share(mine, received):
    return (mine.astype(jnp.float32) + received.astype(jnp.float32)).astype(mine.dtype)


def half_scatter(far_low, far_high, ahead_low, ahead_high, behind_low, behind_high, own):
    low = shift_rows(far_low, 1)
    high = shift_rows(far_high, -1)
    before_high = shift_rows(ahead_high, 1)
    after_low = shift_rows(behind_low, -1)
    before_low = shift_rows(add_share(ahead_low, low), 1)
    after_high = shift_rows(add_share(behind_high, high), -1)
    return [own, before_low, before_high, after_low, after_high]


def layer(
    hidden_states,
    lengths,
    shard_order,
    gain_attn,
    w_query,
    w_key,
    w_value,
    w_out,
    rel_bias,
    gain_ff,
    w_gate,
    w_up,
    w_down,
    gain_final,
    w_reward,
):
    bf16, f32 = jnp.bfloat16, jnp.float32
    shape = jax.ShapeDtypeStruct
    rows, width = hidden_states.shape
    half = rows // 2
    length_all = 4 * rows
    block = w_query.shape[0]
    inner = w_query.shape[1]
    hidden = w_gate.shape[1]
    ids = jnp.stack([lax.axis_index("dp"), lax.axis_index("tensor")]).astype(jnp.int32)
    half_bf = shape((half, width), bf16)
    row_bf = shape((rows, width), bf16)
    row_f32 = shape((rows, width), f32)

    qkv_own = call(
        pack_kernel, [], [w_query, w_key, w_value], [],
        shape((block, 3 * inner), bf16), [], 2 * block * inner, 12 * block * inner,
    )
    low, high = call(
        rms_kernel, [], [hidden_states, gain_attn.reshape(1, width)], [],
        [half_bf, half_bf], [], 4 * rows * width, 6 * rows * width,
    )
    normed = half_gather(low, high)
    qkv = plane_gather_split(qkv_own)
    out_blocks = plane_gather(w_out)
    feed_own = call(
        pack_kernel, [], [w_gate, w_up, w_down], [],
        shape((block, 3 * hidden), bf16), [], 2 * block * hidden, 12 * block * hidden,
    )
    feed = plane_gather_split(feed_own)

    tile = 2 * TILE
    projected = call(
        project_kernel, [shard_order, ids], normed, qkv,
        shape((length_all, 3 * inner), bf16),
        [
            pltpu.VMEM((length_all, width), bf16),
            pltpu.VMEM((3 * inner // tile, width, tile), bf16),
            pltpu.SemaphoreType.DMA((3 * inner // tile,)),
        ],
        6 * length_all * width * inner, 6 * width * inner,
    )

    heads = rel_bias.shape[1]
    relative = jnp.arange(4 * TILE, dtype=jnp.int32) - 2 * TILE
    onehot = (
        bucket_index(relative)[:, None]
        == jnp.arange(rel_bias.shape[0], dtype=jnp.int32)[None, :]
    ).astype(f32)
    bias_table = jnp.dot(onehot, rel_bias, precision=lax.Precision.HIGHEST).T
    context = attention(lengths, projected, bias_table.reshape(heads // 2, 2, 4 * TILE))

    parts = call(
        out_kernel, [shard_order, ids], [context], out_blocks,
        [half_bf] * 6 + [row_bf],
        [
            pltpu.VMEM((length_all, inner), bf16),
            pltpu.VMEM((8, inner, block), bf16),
            pltpu.SemaphoreType.DMA((8,)),
        ],
        2 * length_all * width * inner, 2 * width * inner,
    )
    mid, low, high = call(
        mid_kernel, [],
        [hidden_states, *half_scatter(*parts), gain_ff.reshape(1, width)], [],
        [row_f32, half_bf, half_bf], [], 8 * rows * width, 16 * rows * width,
    )
    normed = half_gather(low, high)

    def feed_forward(pieces):
        count = len(pieces)
        return call(
            functools.partial(feed_kernel, count), [shard_order, ids], pieces, feed,
            [half_bf] * count,
            [
                pltpu.VMEM((count * half, width), bf16),
                pltpu.VMEM((count * half, hidden), bf16),
                pltpu.VMEM((hidden // tile, width, 2 * tile), bf16),
                pltpu.VMEM((8, hidden, block), bf16),
                pltpu.SemaphoreType.DMA((hidden // tile,)),
                pltpu.SemaphoreType.DMA((8,)),
            ],
            6 * count * half * width * hidden, 6 * width * hidden,
        )

    near = feed_forward(normed[:6])
    far = feed_forward(normed[6:])
    own = jnp.concatenate(near[:2])
    shares = half_scatter(far[0], far[1], near[4], near[5], near[2], near[3], own)
    output_rows, pool = call(
        final_kernel, [lengths, ids],
        [mid, *shares, gain_final.reshape(1, width), w_reward.reshape(1, width)], [],
        [row_f32, shape((8, TILE), f32)], [], 8 * rows * width, 16 * rows * width,
    )
    total = pool
    for step in (1, 2):
        total = total + lax.ppermute(total, "tensor", [(i, i ^ step) for i in range(4)])
    reward = total / lengths[0].astype(f32)
    moments = jnp.where(lax.broadcasted_iota(jnp.int32, reward.shape, 0) == 0, reward, reward * reward)
    for mask in (1, 2, 4):
        moments = moments + exchange(moments, mask)
    reward_mean = moments[0, 0] / 8
    reward_var = moments[1, 0] / 8 - reward_mean * reward_mean
    normalized = (reward[0, 0] - reward_mean) / jnp.sqrt(reward_var + 1e-06)
    return (output_rows, jnp.reshape(normalized, (1,)))


def local_fast(*args):
    return layer(*args)


def solution(mesh):
    placed = (
        P(("dp", "tensor"), None),
        P("dp"),
        P(),
        P(),
        P("dp", "tensor"),
        P("dp", "tensor"),
        P("dp", "tensor"),
        P("tensor", "dp"),
        P(None, "tensor"),
        P(),
        P("dp", "tensor"),
        P("dp", "tensor"),
        P("tensor", "dp"),
        P(),
        P(),
    )
    fits = mesh.shape["dp"] == 8 and mesh.shape["tensor"] == 4
    return jax.shard_map(
        local_fast if fits else local_general,
        mesh=mesh,
        in_specs=placed,
        out_specs=(P(("dp", "tensor"), None), P("dp")),
        check_vma=False,
    )
```

profile of v0, /device:TPU:0, one launch (start us, length us, event | category | flops | bytes accessed | tf_op | source)
XLA Modules:
  0.0 276.8 jit_solution(13519374953120892069)
XLA Ops:
  14.8 5.9 %collective-permute-done.refs_2_ = bf16[64,2048]{1,0:T(8,128)(2,1)S(1)} collective-permute-done((bf16[64,2048]{1,0:T(8,128)(2,1)}, bf16[64,2048]{1,0:T(8,128)(2,1)S(1)}, u32[]{:S(2)}, u32[]{:S(2)}) %collective-permute-start) | collective-permute-done | bytes 262176 | tf_op jit(solution)/shard_map/ppermute | solution.py:498
  22.4 3.8 %collective-permute-done.1.refs_3_ = bf16[64,2048]{1,0:T(8,128)(2,1)S(1)} collective-permute-done((bf16[64,2048]{1,0:T(8,128)(2,1)}, bf16[64,2048]{1,0:T(8,128)(2,1)S(1)}, u32[]{:S(2)}, u32[]{:S(2)}) %collective-permute-start.1) | collective-permute-done | bytes 262176 | tf_op jit(solution)/shard_map/ppermute | solution.py:498
  26.3 4.1 %collective-permute-done.2.refs_4_ = bf16[64,2048]{1,0:T(8,128)(2,1)} collective-permute-done((bf16[64,2048]{1,0:T(8,128)(2,1)}, bf16[64,2048]{1,0:T(8,128)(2,1)}, u32[]{:S(2)}, u32[]{:S(2)}) %collective-permute-start.2) | collective-permute-done | bytes 262176 | tf_op jit(solution)/shard_map/ppermute | solution.py:498
  30.9 4.9 %collective-permute-done.3.refs_5_ = bf16[64,2048]{1,0:T(8,128)(2,1)S(1)} collective-permute-done((bf16[64,2048]{1,0:T(8,128)(2,1)}, bf16[64,2048]{1,0:T(8,128)(2,1)S(1)}, u32[]{:S(2)}, u32[]{:S(2)}) %collective-permute-start.3) | collective-permute-done | bytes 262176 | tf_op jit(solution)/shard_map/ppermute | solution.py:498
  39.6 7.3 %collective-permute-start.5 = (bf16[64,2048]{1,0:T(8,128)(2,1)S(1)}, bf16[64,2048]{1,0:T(8,128)(2,1)S(1)}, u32[]{:S(2)}, u32[]{:S(2)}) collective-permute-start(bf16[64,2048]{1,0:T(8,128)(2,1)S(1)} %collective-permute-done.3.refs_5_), channel_id=1, source_target_pairs={{0,3},{1,0},{2,1},{3,2},{4,7},{5,4},{6,5},{7,6},{8,11},{9,8},{10,9... | collective-permute-start | bytes 786440 | tf_op jit(solution)/shard_map/ppermute | solution.py:498
  54.0 3.5 %collective-permute-done.5.refs_7_ = bf16[64,2048]{1,0:T(8,128)(2,1)S(1)} collective-permute-done((bf16[64,2048]{1,0:T(8,128)(2,1)S(1)}, bf16[64,2048]{1,0:T(8,128)(2,1)S(1)}, u32[]{:S(2)}, u32[]{:S(2)}) %collective-permute-start.5) | collective-permute-done | bytes 262176 | tf_op jit(solution)/shard_map/ppermute | solution.py:498
  69.0 9.0 %shard_map.160.q_ref.k_ref.v_ref = bf16[512,1536]{1,0:T(8,128)(2,1)} custom-call(s32[8]{0:T(128)} %order.7, s32[2]{0:T(128)} %pad_add_fusion.ids, bf16[64,2048]{1,0:T(8,128)(2,1)} %get-tuple-element.24.refs_0_, bf16[64,2048]{1,0:T(8,128)(2,1)} %get-tuple-element.25.refs_1_, bf16[64,2048]{1,0:T(8,128)(2,1)} %copy-done.22, bf16[64,2048]{1,0:T(8,128)(2,1)} %copy-done.23, ...), custom_call_target="tpu_custom_call" | custom-call | flops 3221225472 | bytes 6291456 | tf_op jit(solution)/shard_map/pallas_call | solution.py:481
  78.0 13.5 %attention.1.context = bf16[512,512]{1,0:T(8,128)(2,1)} custom-call(s32[1]{0:T(128)S(6)} %copy.17.length_ref.length, bf16[512,1536]{1,0:T(8,128)(2,1)} %shard_map.160.q_ref.k_ref.v_ref, bf16[512,1536]{1,0:T(8,128)(2,1)} %shard_map.160.q_ref.k_ref.v_ref, bf16[512,1536]{1,0:T(8,128)(2,1)} %shard_map.160.q_ref.k_ref.v_ref, f32[4,2,512]{2,1,0:T(2,128)} %reshape.65.bias_ref), custom_call_target="tpu_custom_call" | custom-call | flops 2147483648 | bytes 2097152 | tf_op jit(solution)/shard_map/attention/pallas_call | solution.py:162
  91.6 6.9 %shard_map.161 = (bf16[64,2048]{1,0:T(8,128)(2,1)}, bf16[64,2048]{1,0:T(8,128)(2,1)}, bf16[64,2048]{1,0:T(8,128)(2,1)}, bf16[64,2048]{1,0:T(8,128)(2,1)}, bf16[6...) custom-call(s32[8]{0:T(128)} %order.7, s32[2]{0:T(128)} %pad_add_fusion.ids, ...), custom_call_target="tpu_custom_call" | custom-call | flops 1073741824 | bytes 2097152 | tf_op jit(solution)/shard_map/pallas_call | solution.py:481
  100.9 8.8 %collective-permute-done.22 = bf16[64,2048]{1,0:T(8,128)(2,1)S(1)} collective-permute-done((bf16[64,2048]{1,0:T(8,128)(2,1)}, bf16[64,2048]{1,0:T(8,128)(2,1)S(1)}, u32[]{:S(2)}, u32[]{:S(2)}) %collective-permute-start.22) | collective-permute-done | bytes 262176 | tf_op jit(solution)/shard_map/ppermute | solution.py:498
  111.7 8.7 %collective-permute-done.26 = bf16[64,2048]{1,0:T(8,128)(2,1)S(1)} collective-permute-done((bf16[64,2048]{1,0:T(8,128)(2,1)}, bf16[64,2048]{1,0:T(8,128)(2,1)S(1)}, u32[]{:S(2)}, u32[]{:S(2)}) %collective-permute-start.26) | collective-permute-done | bytes 262176 | tf_op jit(solution)/shard_map/ppermute | solution.py:498
  130.3 5.0 %collective-permute-done.25.refs_3_ = bf16[64,2048]{1,0:T(8,128)(2,1)S(1)} collective-permute-done((bf16[64,2048]{1,0:T(8,128)(2,1)}, bf16[64,2048]{1,0:T(8,128)(2,1)S(1)}, u32[]{:S(2)}, u32[]{:S(2)}) %collective-permute-start.25) | collective-permute-done | bytes 262176 | tf_op jit(solution)/shard_map/ppermute | solution.py:498
  136.3 3.8 %collective-permute-done.27.refs_4_ = bf16[64,2048]{1,0:T(8,128)(2,1)S(1)} collective-permute-done((bf16[64,2048]{1,0:T(8,128)(2,1)S(1)}, bf16[64,2048]{1,0:T(8,128)(2,1)S(1)}, u32[]{:S(2)}, u32[]{:S(2)}) %collective-permute-start.27) | collective-permute-done | bytes 262176 | tf_op jit(solution)/shard_map/ppermute | solution.py:498
  145.5 9.3 %collective-permute-done.37.refs_12_.refs_8_ = bf16[128,3840]{1,0:T(8,128)(2,1)S(1)} collective-permute-done((bf16[128,3840]{1,0:T(8,128)(2,1)}, bf16[128,3840]{1,0:T(8,128)(2,1)S(1)}, u32[]{:S(2)}, u32[]{:S(2)}) %collective-permute-start.37) | collective-permute-done | bytes 983072 | tf_op jit(solution)/shard_map/ppermute | solution.py:502
  154.8 9.1 %collective-permute-done.38.refs_13_.refs_9_ = bf16[128,3840]{1,0:T(8,128)(2,1)} collective-permute-done((bf16[128,3840]{1,0:T(8,128)(2,1)}, bf16[128,3840]{1,0:T(8,128)(2,1)}, u32[]{:S(2)}, u32[]{:S(2)}) %collective-permute-start.38) | collective-permute-done | bytes 983072 | tf_op jit(solution)/shard_map/ppermute | solution.py:502
  165.8 7.0 %collective-permute-done.31.refs_5_ = bf16[64,2048]{1,0:T(8,128)(2,1)S(1)} collective-permute-done((bf16[64,2048]{1,0:T(8,128)(2,1)}, bf16[64,2048]{1,0:T(8,128)(2,1)S(1)}, u32[]{:S(2)}, u32[]{:S(2)}) %collective-permute-start.31) | collective-permute-done | bytes 262176 | tf_op jit(solution)/shard_map/ppermute | solution.py:498
  173.3 9.3 %collective-permute-done.41.refs_0_ = bf16[64,2048]{1,0:T(8,128)(2,1)S(1)} collective-permute-done((bf16[64,2048]{1,0:T(8,128)(2,1)S(1)}, bf16[64,2048]{1,0:T(8,128)(2,1)S(1)}, u32[]{:S(2)}, u32[]{:S(2)}) %collective-permute-start.41) | collective-permute-done | bytes 262176 | tf_op jit(solution)/shard_map/ppermute | solution.py:498
  184.3 5.3 %collective-permute-done.42.refs_1_ = bf16[64,2048]{1,0:T(8,128)(2,1)S(1)} collective-permute-done((bf16[64,2048]{1,0:T(8,128)(2,1)S(1)}, bf16[64,2048]{1,0:T(8,128)(2,1)S(1)}, u32[]{:S(2)}, u32[]{:S(2)}) %collective-permute-start.42) | collective-permute-done | bytes 262176 | tf_op jit(solution)/shard_map/ppermute | solution.py:498
  189.6 4.1 %collective-permute-start.30 = (bf16[64,2048]{1,0:T(8,128)(2,1)}, bf16[64,2048]{1,0:T(8,128)(2,1)}, u32[]{:S(2)}, u32[]{:S(2)}) collective-permute-start(bf16[64,2048]{1,0:T(8,128)(2,1)} %get-tuple-element.34.refs_0_), channel_id=1, source_target_pairs={{0,3},{1,0},{2,1},{3,2},{4,7},{5,4},{6,5},{7,6},{8,11},{9,8},{10,9... | collective-permute-start | bytes 786440 | tf_op jit(solution)/shard_map/ppermute | solution.py:498
  195.7 10.8 %shard_map.165 = (bf16[64,2048]{1,0:T(8,128)(2,1)}, bf16[64,2048]{1,0:T(8,128)(2,1)}) custom-call(s32[8]{0:T(128)} %order.7, s32[2]{0:T(128)} %pad_add_fusion.ids, bf16[64,2048]{1,0:T(8,128)(2,1)} %copy-done.5, bf16[64,2048]{1,0:T(8,128)(2,1)} %copy-done.6, bf16[256,3840]{1,0:T(8,128)(2,1)} %shard_map.163.refs_6_.refs_2_, ...), custom_call_target="tpu_custom_call" | custom-call | flops 2013265920 | bytes 15728640 | tf_op jit(solution)/shard_map/pallas_call | solution.py:481
  206.6 13.8 %shard_map.164 = (bf16[64,2048]{1,0:T(8,128)(2,1)}, bf16[64,2048]{1,0:T(8,128)(2,1)}, bf16[64,2048]{1,0:T(8,128)(2,1)}, bf16[64,2048]{1,0:T(8,128)(2,1)}, bf16[6...) custom-call(s32[8]{0:T(128)} %order.7, s32[2]{0:T(128)} %pad_add_fusion.ids, bf16[64,2048]{1,0:T(8,128)(2,1)} %get-tuple-element.34.refs_0_, ...), custom_call_target="tpu_custom_call" | custom-call | flops 6039797760 | bytes 15728640 | tf_op jit(solution)/shard_map/pallas_call | solution.py:481
  227.5 12.6 %collective-permute-done.47 = bf16[64,2048]{1,0:T(8,128)(2,1)S(1)} collective-permute-done((bf16[64,2048]{1,0:T(8,128)(2,1)S(1)}, bf16[64,2048]{1,0:T(8,128)(2,1)S(1)}, u32[]{:S(2)}, u32[]{:S(2)}) %collective-permute-start.47) | collective-permute-done | bytes 262176 | tf_op jit(solution)/shard_map/ppermute | solution.py:498
  251.2 3.6 %shard_map.166 = (f32[128,2048]{1,0:T(8,128)}, f32[8,128]{1,0:T(8,128)}) custom-call(s32[1]{0:T(128)S(6)} %copy.17.length_ref.length, s32[2]{0:T(128)} %pad_add_fusion.ids, f32[128,2048]{1,0:T(8,128)} %get-tuple-element.33.x_ref, bf16[128,2048]{1,0:T(8,128)(2,1)} %pad_maximum_fusion.refs_0_, bf16[64,2048]{1,0:T(8,128)(2,1)} %copy-done.12, ...), custom_call_target="tpu_custom_call" | custom-call | flops 2097152 | bytes 4194304 | tf_op jit(solution)/shard_map/pallas_call | solution.py:481
  259.6 4.1 %collective-permute-done.50 = f32[8,128]{1,0:T(8,128)S(1)} collective-permute-done((f32[8,128]{1,0:T(8,128)S(1)}, f32[8,128]{1,0:T(8,128)S(1)}, u32[]{:S(2)}, u32[]{:S(2)}) %collective-permute-start.50) | collective-permute-done | bytes 4128 | tf_op jit(solution)/shard_map/ppermute | solution.py:663
  (179 shorter events, 96.7 us)
Async XLA Ops:
  2.7 36.3 %collective-permute-start.7 = (bf16[256,1536]{1,0:T(8,128)(2,1)}, bf16[256,1536]{1,0:T(8,128)(2,1)S(1)}, u32[]{:S(2)}, u32[]{:S(2)}) collective-permute-start(bf16[256,1536]{1,0:T(8,128)(2,1)} %shard_map.159.refs_8_), channel_id=1, source_target_pairs={{0,8},{4,12},{8,0},{12,4},{16,24},{20,28},{24,16},{28,20},{1,9},{5... | collective-permute-start | bytes 2359304 | tf_op jit(solution)/shard_map/ppermute | solution.py:502
  5.7 33.9 %collective-permute-start.9 = (bf16[256,1536]{1,0:T(8,128)(2,1)}, bf16[256,1536]{1,0:T(8,128)(2,1)S(1)}, u32[]{:S(2)}, u32[]{:S(2)}) collective-permute-start(bf16[256,1536]{1,0:T(8,128)(2,1)} %shard_map.159.refs_8_), channel_id=1, source_target_pairs={{0,16},{4,20},{8,24},{12,28},{16,0},{20,4},{24,8},{28,12},{1,17},{... | collective-permute-start | bytes 2359304 | tf_op jit(solution)/shard_map/ppermute | solution.py:502
  12.6 17.8 %collective-permute-start.2 = (bf16[64,2048]{1,0:T(8,128)(2,1)}, bf16[64,2048]{1,0:T(8,128)(2,1)}, u32[]{:S(2)}, u32[]{:S(2)}) collective-permute-start(bf16[64,2048]{1,0:T(8,128)(2,1)} %get-tuple-element.24.refs_0_), channel_id=1, source_target_pairs={{0,3},{1,0},{2,1},{3,2},{4,7},{5,4},{6,5},{7,6},{8,11},{9,8},{10,9... | collective-permute-start | bytes 786440 | tf_op jit(solution)/shard_map/ppermute | solution.py:498
  35.8 28.5 %collective-permute-start.6 = (bf16[256,1536]{1,0:T(8,128)(2,1)}, bf16[256,1536]{1,0:T(8,128)(2,1)S(1)}, u32[]{:S(2)}, u32[]{:S(2)}) collective-permute-start(bf16[256,1536]{1,0:T(8,128)(2,1)} %shard_map.159.refs_8_), channel_id=1, source_target_pairs={{0,4},{4,0},{8,12},{12,8},{16,20},{20,16},{24,28},{28,24},{1,5},{5... | collective-permute-start | bytes 2359304 | tf_op jit(solution)/shard_map/ppermute | solution.py:502
  39.6 17.9 %collective-permute-start.5 = (bf16[64,2048]{1,0:T(8,128)(2,1)S(1)}, bf16[64,2048]{1,0:T(8,128)(2,1)S(1)}, u32[]{:S(2)}, u32[]{:S(2)}) collective-permute-start(bf16[64,2048]{1,0:T(8,128)(2,1)S(1)} %collective-permute-done.3.refs_5_), channel_id=1, source_target_pairs={{0,3},{1,0},{2,1},{3,2},{4,7},{5,4},{6,5},{7,6},{8,11},{9,8},{10,9... | collective-permute-start | bytes 786440 | tf_op jit(solution)/shard_map/ppermute | solution.py:498
  64.4 59.2 %collective-permute-start.33 = (bf16[256,3840]{1,0:T(8,128)(2,1)}, bf16[256,3840]{1,0:T(8,128)(2,1)}, u32[]{:S(2)}, u32[]{:S(2)}) collective-permute-start(bf16[256,3840]{1,0:T(8,128)(2,1)} %shard_map.163.refs_6_.refs_2_), channel_id=1, source_target_pairs={{0,8},{4,12},{8,0},{12,4},{16,24},{20,28},{24,16},{28,20},{1,9},{5... | collective-permute-start | bytes 5898248 | tf_op jit(solution)/shard_map/ppermute | solution.py:502
  67.9 58.0 %collective-permute-start.35 = (bf16[256,3840]{1,0:T(8,128)(2,1)}, bf16[256,3840]{1,0:T(8,128)(2,1)}, u32[]{:S(2)}, u32[]{:S(2)}) collective-permute-start(bf16[256,3840]{1,0:T(8,128)(2,1)} %shard_map.163.refs_6_.refs_2_), channel_id=1, source_target_pairs={{0,16},{4,20},{8,24},{12,28},{16,0},{20,4},{24,8},{28,12},{1,17},{... | collective-permute-start | bytes 5898248 | tf_op jit(solution)/shard_map/ppermute | solution.py:502
  68.4 23.2 %collective-permute-start.17 = (bf16[512,256]{1,0:T(8,128)(2,1)S(1)}, bf16[512,256]{1,0:T(8,128)(2,1)}, u32[]{:S(2)}, u32[]{:S(2)}) collective-permute-start(bf16[512,256]{1,0:T(8,128)(2,1)S(1)} %copy-done.21), channel_id=1, source_target_pairs={{0,4},{4,0},{8,12},{12,8},{16,20},{20,16},{24,28},{28,24},{1,5},{5... | collective-permute-start | bytes 786440 | tf_op jit(solution)/shard_map/ppermute | solution.py:502
  68.4 23.2 %collective-permute-start.19 = (bf16[512,256]{1,0:T(8,128)(2,1)}, bf16[512,256]{1,0:T(8,128)(2,1)}, u32[]{:S(2)}, u32[]{:S(2)}) collective-permute-start(bf16[512,256]{1,0:T(8,128)(2,1)} %copy-done.24), channel_id=1, source_target_pairs={{0,4},{4,0},{8,12},{12,8},{16,20},{20,16},{24,28},{28,24},{1,5},{5... | collective-permute-start | bytes 786440 | tf_op jit(solution)/shard_map/ppermute | solution.py:502
  68.9 22.7 %collective-permute-start.21 = (bf16[512,256]{1,0:T(8,128)(2,1)}, bf16[512,256]{1,0:T(8,128)(2,1)}, u32[]{:S(2)}, u32[]{:S(2)}) collective-permute-start(bf16[512,256]{1,0:T(8,128)(2,1)} %copy-done.26), channel_id=1, source_target_pairs={{0,4},{4,0},{8,12},{12,8},{16,20},{20,16},{24,28},{28,24},{1,5},{5... | collective-permute-start | bytes 786440 | tf_op jit(solution)/shard_map/ppermute | solution.py:502
  99.1 46.0 %collective-permute-start.32 = (bf16[256,3840]{1,0:T(8,128)(2,1)S(1)}, bf16[256,3840]{1,0:T(8,128)(2,1)}, u32[]{:S(2)}, u32[]{:S(2)}) collective-permute-start(bf16[256,3840]{1,0:T(8,128)(2,1)S(1)} %copy-done.1), channel_id=1, source_target_pairs={{0,4},{4,0},{8,12},{12,8},{16,20},{20,16},{24,28},{28,24},{1,5},{5... | collective-permute-start | bytes 5898248 | tf_op jit(solution)/shard_map/ppermute | solution.py:502
  99.1 22.9 %collective-permute-start.24 = (bf16[64,2048]{1,0:T(8,128)(2,1)}, bf16[64,2048]{1,0:T(8,128)(2,1)S(1)}, u32[]{:S(2)}, u32[]{:S(2)}) collective-permute-start(bf16[64,2048]{1,0:T(8,128)(2,1)} %get-tuple-element.29), channel_id=1, source_target_pairs={{0,1},{1,2},{2,3},{3,0},{4,5},{5,6},{6,7},{7,4},{8,9},{9,10},{10,1... | collective-permute-start | bytes 786440 | tf_op jit(solution)/shard_map/ppermute | solution.py:498
  125.9 63.7 %collective-permute-start.34 = (bf16[256,3840]{1,0:T(8,128)(2,1)}, bf16[256,3840]{1,0:T(8,128)(2,1)}, u32[]{:S(2)}, u32[]{:S(2)}) collective-permute-start(bf16[256,3840]{1,0:T(8,128)(2,1)} %collective-permute-done.33.refs_8_.refs_4_), channel_id=1, source_target_pairs={{0,4},{4,0},{8,12},{12,8},{16,20},{20,16},{24,28},{28,24},{1,5},{5... | collective-permute-start | bytes 5898248 | tf_op jit(solution)/shard_map/ppermute | solution.py:502
  135.4 19.4 %collective-permute-start.37 = (bf16[128,3840]{1,0:T(8,128)(2,1)}, bf16[128,3840]{1,0:T(8,128)(2,1)S(1)}, u32[]{:S(2)}, u32[]{:S(2)}) collective-permute-start(bf16[128,3840]{1,0:T(8,128)(2,1)} %slice.30), channel_id=1, source_target_pairs={{0,8},{4,12},{8,0},{12,4},{16,24},{20,28},{24,16},{28,20},{1,9},{5... | collective-permute-start | bytes 2949128 | tf_op jit(solution)/shard_map/ppermute | solution.py:502
  136.3 57.5 %collective-permute-start.36 = (bf16[256,3840]{1,0:T(8,128)(2,1)}, bf16[256,3840]{1,0:T(8,128)(2,1)}, u32[]{:S(2)}, u32[]{:S(2)}) collective-permute-start(bf16[256,3840]{1,0:T(8,128)(2,1)} %collective-permute-done.35.refs_10_.refs_6_), channel_id=1, source_target_pairs={{0,4},{4,0},{8,12},{12,8},{16,20},{20,16},{24,28},{28,24},{1,5},{5... | collective-permute-start | bytes 5898248 | tf_op jit(solution)/shard_map/ppermute | solution.py:502
  140.8 23.1 %collective-permute-start.38 = (bf16[128,3840]{1,0:T(8,128)(2,1)}, bf16[128,3840]{1,0:T(8,128)(2,1)}, u32[]{:S(2)}, u32[]{:S(2)}) collective-permute-start(bf16[128,3840]{1,0:T(8,128)(2,1)} %slice.31), channel_id=1, source_target_pairs={{0,16},{4,20},{8,24},{12,28},{16,0},{20,4},{24,8},{28,12},{1,17},{... | collective-permute-start | bytes 2949128 | tf_op jit(solution)/shard_map/ppermute | solution.py:502
  145.1 18.9 %collective-permute-start.28 = (bf16[64,2048]{1,0:T(8,128)(2,1)}, bf16[64,2048]{1,0:T(8,128)(2,1)S(1)}, u32[]{:S(2)}, u32[]{:S(2)}) collective-permute-start(bf16[64,2048]{1,0:T(8,128)(2,1)} %get-tuple-element.34.refs_0_), channel_id=1, source_target_pairs={{0,1},{1,2},{2,3},{3,0},{4,5},{5,6},{6,7},{7,4},{8,9},{9,10},{10,1... | collective-permute-start | bytes 786440 | tf_op jit(solution)/shard_map/ppermute | solution.py:498
  154.8 39.0 %collective-permute-start.39 = (bf16[128,3840]{1,0:T(8,128)(2,1)S(1)}, bf16[128,3840]{1,0:T(8,128)(2,1)S(1)}, u32[]{:S(2)}, u32[]{:S(2)}) collective-permute-start(bf16[128,3840]{1,0:T(8,128)(2,1)S(1)} %collective-permute-done.37.refs_12_.refs_8_), channel_id=1, source_target_pairs={{0,4},{4,0},{8,12},{12,8},{16,20},{20,16},{24,28},{28,24},{1,5},{5... | collective-permute-start | bytes 2949128 | tf_op jit(solution)/shard_map/ppermute | solution.py:502
  163.9 29.9 %collective-permute-start.40 = (bf16[128,3840]{1,0:T(8,128)(2,1)}, bf16[128,3840]{1,0:T(8,128)(2,1)S(1)}, u32[]{:S(2)}, u32[]{:S(2)}) collective-permute-start(bf16[128,3840]{1,0:T(8,128)(2,1)} %collective-permute-done.38.refs_13_.refs_9_), channel_id=1, source_target_pairs={{0,4},{4,0},{8,12},{12,8},{16,20},{20,16},{24,28},{28,24},{1,5},{5... | collective-permute-start | bytes 2949128 | tf_op jit(solution)/shard_map/ppermute | solution.py:502
  189.6 17.0 %collective-permute-start.30 = (bf16[64,2048]{1,0:T(8,128)(2,1)}, bf16[64,2048]{1,0:T(8,128)(2,1)}, u32[]{:S(2)}, u32[]{:S(2)}) collective-permute-start(bf16[64,2048]{1,0:T(8,128)(2,1)} %get-tuple-element.34.refs_0_), channel_id=1, source_target_pairs={{0,3},{1,0},{2,1},{3,2},{4,7},{5,4},{6,5},{7,6},{8,11},{9,8},{10,9... | collective-permute-start | bytes 786440 | tf_op jit(solution)/shard_map/ppermute | solution.py:498
  206.6 19.8 %collective-permute-start.43 = (bf16[64,2048]{1,0:T(8,128)(2,1)}, bf16[64,2048]{1,0:T(8,128)(2,1)S(1)}, u32[]{:S(2)}, u32[]{:S(2)}) collective-permute-start(bf16[64,2048]{1,0:T(8,128)(2,1)} %get-tuple-element.39), channel_id=1, source_target_pairs={{0,1},{1,2},{2,3},{3,0},{4,5},{5,6},{6,7},{7,4},{8,9},{9,10},{10,1... | collective-permute-start | bytes 786440 | tf_op jit(solution)/shard_map/ppermute | solution.py:498
  220.5 25.3 %collective-permute-start.45 = (bf16[64,2048]{1,0:T(8,128)(2,1)}, bf16[64,2048]{1,0:T(8,128)(2,1)S(1)}, u32[]{:S(2)}, u32[]{:S(2)}) collective-permute-start(bf16[64,2048]{1,0:T(8,128)(2,1)} %get-tuple-element.40), channel_id=1, source_target_pairs={{0,1},{1,2},{2,3},{3,0},{4,5},{5,6},{6,7},{7,4},{8,9},{9,10},{10,1... | collective-permute-start | bytes 786440 | tf_op jit(solution)/shard_map/ppermute | solution.py:498
  221.6 24.2 %collective-permute-start.46 = (bf16[64,2048]{1,0:T(8,128)(2,1)}, bf16[64,2048]{1,0:T(8,128)(2,1)S(1)}, u32[]{:S(2)}, u32[]{:S(2)}) collective-permute-start(bf16[64,2048]{1,0:T(8,128)(2,1)} %get-tuple-element.41), channel_id=1, source_target_pairs={{0,3},{1,0},{2,1},{3,2},{4,7},{5,4},{6,5},{7,6},{8,11},{9,8},{10,9... | collective-permute-start | bytes 786440 | tf_op jit(solution)/shard_map/ppermute | solution.py:498
  227.4 19.8 %collective-permute-start.44 = (bf16[64,2048]{1,0:T(8,128)(2,1)S(1)}, bf16[64,2048]{1,0:T(8,128)(2,1)S(1)}, u32[]{:S(2)}, u32[]{:S(2)}) collective-permute-start(bf16[64,2048]{1,0:T(8,128)(2,1)S(1)} %add_convert_fusion.1), channel_id=1, source_target_pairs={{0,1},{1,2},{2,3},{3,0},{4,5},{5,6},{6,7},{7,4},{8,9},{9,10},{10,1... | collective-permute-start | bytes 786440 | tf_op jit(solution)/shard_map/ppermute | solution.py:498
  (62 other events, 751.4 us)
where the time goes:
time: 278 us; the launch traced here: 277 us
  waiting for transfers between devices  130 us (47%)
  Pallas kernels  67.9 us (24%)
  starting transfers between devices  55.8 us (20%)
  local copies, waits for them, and re-layouts  9.49 us (3%)
  other arithmetic  7.31 us (3%)
  between operations  5.7 us (2%)
    ppermute x24, waiting for transfers between devices, shift_rows(): return lax.ppermute(block, 'tensor', ring_pairs(step))  90.2 us
    pallas_call x9, Pallas kernels, call(): pl.pallas_call(kernel, out_shape=out_list, grid_spec=pltpu.PrefetchScalar...  54.4 us
    ppermute x24, starting transfers between devices, shift_rows(): return lax.ppermute(block, 'tensor', ring_pairs(step))  40.2 us
    ppermute x28, waiting for transfers between devices, exchange(): return lax.ppermute(block, 'dp', [(i, i ^ mask) for i in range(8)])  33.3 us
    ppermute x28, starting transfers between devices, exchange(): return lax.ppermute(block, 'dp', [(i, i ^ mask) for i in range(8)])  14 us
    pallas_call x1, Pallas kernels, attention(): pl.pallas_call(attention_kernel, out_shape=jax.ShapeDtypeStruct((span, in...  13.5 us
    ppermute x2, waiting for transfers between devices, layer(): lax.ppermute(total, 'tensor', [(i, i ^ step) for i in range(4)])  6.77 us
  transfers between devices with their start and end apart: 54, of which 27 were waited for; matrix products, arithmetic and copies ran while one was open for 5% of the time, Pallas kernels for 23%

commit v1 on v0

--- a/solution.py
+++ b/solution.py
@@ -109,50 +109,43 @@
 
 
 def attention_kernel(length_ref, q_ref, k_ref, v_ref, bias_ref, o_ref):
-    span = q_ref.shape[0]
-    lanes = q_ref.shape[1]
+    span, lanes = q_ref.shape
     blocks = span // TILE
     length = length_ref[0]
     keys = k_ref[...]
     values = v_ref[...]
-    valid = lax.broadcasted_iota(jnp.int32, (1, span), 1) < length
-    first_head = lax.broadcasted_iota(jnp.int32, (1, lanes), 1) < DK
-    contexts = []
+    masked = jnp.where(lax.broadcasted_iota(jnp.int32, (1, span), 1) < length, 0.0, -1e30)
+    first = lax.broadcasted_iota(jnp.int32, (1, lanes), 1) < DK
+    one = jnp.ones_like(values)
+    sums = []
     for head in range(2):
         table = bias_ref[0, head : head + 1, :]
-        near = pltpu.roll(
-            jnp.broadcast_to(table, (TILE, 4 * TILE)), 0, 1, stride=1, stride_axis=0
-        )
-        own = first_head if head == 0 else jnp.logical_not(first_head)
-        far_left = jnp.broadcast_to(table[:, 1:2], (TILE, TILE))
-        far_right = jnp.broadcast_to(table[:, 4 * TILE - 1 :], (TILE, TILE))
-        pieces = []
+        near = pltpu.roll(jnp.broadcast_to(table, (TILE, 4 * TILE)), 0, 1, stride=1, stride_axis=0)
+        own = first if head == 0 else jnp.logical_not(first)
+        with_ones = jnp.where(own, values, one)
+        far_left, far_right = table[:, 1:2], table[:, 4 * TILE - 1 :]
+        heads = []
         for block in range(blocks):
             queries = q_ref[block * TILE : (block + 1) * TILE, :]
             queries = jnp.where(own, queries, jnp.zeros_like(queries))
-            scores = lax.dot_general(
-                queries, keys, (((1,), (1,)), ((), ())), preferred_element_type=jnp.float32
-            )
-            bias = []
+            scores = lax.dot_general(queries, keys, (((1,), (1,)), ((), ())), preferred_element_type=jnp.float32)
+            pieces = []
             for other in range(blocks):
+                at = slice(other * TILE, (other + 1) * TILE)
                 delta = other - block
-                if delta < -1:
-                    bias.append(far_left)
-                elif delta > 1:
-                    bias.append(far_right)
+                if abs(delta) > 1:
+                    bias = masked[:, at] + (far_left if delta < 0 else far_right)
+                    pieces.append(scores[:, at] + bias)
                 else:
-                    bias.append(near[:, (delta + 2) * TILE : (delta + 3) * TILE])
-            scores = jnp.where(valid, scores + jnp.concatenate(bias, axis=1), -1e30)
-            top = jnp.max(scores, axis=-1, keepdims=True)
-            weights = jnp.exp(scores - top)
-            total = jnp.sum(weights, axis=-1, keepdims=True)
-            soft = (weights / total).astype(jnp.bfloat16)
-            pieces.append(jnp.dot(soft, values, preferred_element_type=jnp.float32))
-        contexts.append(pieces)
+                    pieces.append(scores[:, at] + near[:, (delta + 2) * TILE : (delta + 3) * TILE] + masked[:, at])
+            top = jnp.max(functools.reduce(jnp.maximum, pieces), axis=-1, keepdims=True)
+            soft = jnp.concatenate([jnp.exp(p - top).astype(jnp.bfloat16) for p in pieces], axis=1)
+            heads.append(jnp.dot(soft, with_ones, preferred_element_type=jnp.float32))
+        sums.append(heads)
     for block in range(blocks):
-        o_ref[block * TILE : (block + 1) * TILE, :] = jnp.where(
-            first_head, contexts[0][block], contexts[1][block]
-        ).astype(o_ref.dtype)
+        zero, last = sums[0][block], sums[1][block]
+        total = pltpu.roll(jnp.where(first, last, zero), DK, 1)
+        o_ref[block * TILE : (block + 1) * TILE, :] = (jnp.where(first, zero, last) / total).astype(o_ref.dtype)
 
 
 def attention(length, projected, bias_table):
@@ -287,13 +280,39 @@
     return order[lax.bitwise_xor(ids[0], jnp.int32(mask))]
 
 
-PARTS = ((0, 0), (1, 0), (2, 0), (3, 0), (4, 0), (5, 0), (6, 0), (6, 1), (7, 0), (7, 1))
-
-
-def placed_rows(order, ids, blocks, block):
-    for ref, (mask, part) in zip(blocks, PARTS):
-        start = true_block(order, ids, mask) * block + part * (block // 2)
-        yield ref, pl.multiple_of(start, block // 2)
+def spans(tiles):
+    cut = (tiles + 1) // 2
+    whole_blocks = [(mask, 0, tiles) for mask in range(6)]
+    return whole_blocks + [(mask, *ends) for mask in (6, 7) for ends in ((0, cut), (cut, tiles))]
+
+
+def fetch(order, ids, blocks, tiles, low, high, target, sem):
+    for ref, (mask, first, last) in zip(blocks, spans(tiles)):
+        start, stop = max(low, first), min(high, last)
+        if start < stop:
+            pltpu.make_async_copy(
+                ref.at[pl.ds(start - first, stop - start)],
+                target(true_block(order, ids, mask), start, stop - start),
+                sem,
+            ).start()
+
+
+def into_rows(held, offset):
+    block = held.shape[2]
+
+    def target(where_to, start, count):
+        rows = pl.ds(pl.multiple_of(where_to * block, block), block)
+        return held.at[pl.ds(start - offset, count), rows, :]
+
+    return target
+
+
+def into_blocks(held, offset):
+    return lambda where_to, start, count: held.at[where_to, pl.ds(start - offset, count)]
+
+
+def arrived(part, sem):
+    pltpu.make_async_copy(part, part, sem).wait()
 
 
 def rms_kernel(x_ref, gain_ref, low_ref, high_ref):
@@ -307,47 +326,35 @@
 
 def pack_kernel(*refs):
     *sources, out = refs
-    rows, at = out.shape[0], 0
-    step = 2 * TILE
-    wide = [s for s in sources if s.shape[0] == rows]
-    tall = [s for s in sources if s.shape[0] != rows]
-    if tall:
-        for j in range(wide[0].shape[1] // step):
-            for s in wide:
-                out[:, at : at + step] = s[:, j * step : (j + 1) * step]
-                at += step
-        for s in tall:
-            for j in range(s.shape[0] // rows):
-                out[:, at : at + s.shape[1]] = s[j * rows : (j + 1) * rows, :]
-                at += s.shape[1]
-    else:
-        for s in wide:
-            out[:, at : at + s.shape[1]] = s[...]
-            at += s.shape[1]
+    _, rows, wide = out.shape
+    at = 0
+    for s in sources:
+        for i in range(s.shape[0] // rows):
+            for j in range(s.shape[1] // wide):
+                out[at] = s[i * rows : (i + 1) * rows, j * wide : (j + 1) * wide]
+                at += 1
 
 
 def project_kernel(order, ids, *refs):
     pieces = refs[:8]
     blocks = refs[8:18]
     out, x_all, w_all, sems = refs[18:]
-    tiles, depth, wide = w_all.shape
-    for j in range(tiles):
-        for ref, start in placed_rows(order, ids, blocks, depth // 8):
-            pltpu.make_async_copy(
-                ref.at[:, pl.ds(j * wide, wide)],
-                w_all.at[j, pl.ds(start, ref.shape[0]), :],
-                sems.at[j],
-            ).start()
+    tiles, _, wide = w_all.shape
+    stages = sems.shape[0]
+    each = tiles // stages
+    for g in range(stages):
+        fetch(
+            order, ids, blocks, tiles, g * each, (g + 1) * each, into_rows(w_all, 0), sems.at[g]
+        )
     rows = pieces[0].shape[0]
     for slot, shift in enumerate((0, 3, 1, 2)):
         base = slot_row(ids, shift, 2 * rows)
         put(x_all, base, pieces[2 * slot][...])
         put(x_all, base + rows, pieces[2 * slot + 1][...])
-
-    @pl.loop(0, tiles)
-    def _(j):
-        pltpu.make_async_copy(w_all.at[j], w_all.at[j], sems.at[j]).wait()
-        out[:, pl.ds(pl.multiple_of(j * wide, wide), wide)] = jnp.dot(
+    for j in range(tiles):
+        if j % each == 0:
+            arrived(w_all.at[pl.ds(j, each)], sems.at[j // each])
+        out[:, j * wide : (j + 1) * wide] = jnp.dot(
             x_all[...], w_all[j], preferred_element_type=jnp.float32
         ).astype(out.dtype)
 
@@ -382,52 +389,39 @@
     return 0.5 * v * (1.0 + jnp.tanh(0.7978845608028654 * (v + 0.044715 * (v * v * v))))
 
 
-def feed_kernel(count, order, ids, *refs):
-    pieces = refs[:count]
-    blocks = refs[count : count + 10]
-    outs = refs[count + 10 : 2 * count + 10]
-    x_all, hidden, first, second, sem_first, sem_second = refs[2 * count + 10 :]
-    tiles, depth, wide = first.shape
-    block = depth // 8
-    unit = wide // 2
-    for j in range(tiles):
-        for ref, start in placed_rows(order, ids, blocks, block):
-            pltpu.make_async_copy(
-                ref.at[:, pl.ds(j * wide, wide)],
-                first.at[j, pl.ds(start, ref.shape[0]), :],
-                sem_first.at[j],
-            ).start()
-    for ref, (mask, part) in zip(blocks, PARTS):
-        where_to = true_block(order, ids, mask)
-        for j in range(second.shape[1] // block):
-            pltpu.make_async_copy(
-                ref.at[:, pl.ds(tiles * wide + j * block, block)],
-                second.at[
-                    where_to, pl.ds(j * block + part * (block // 2), ref.shape[0]), :
-                ],
-                sem_second.at[where_to],
-            ).start()
+def feed_kernel(order, ids, *refs):
+    pieces = refs[:8]
+    blocks = refs[8:18]
+    outs = refs[18:25]
+    x_all, hidden, gate, up, down, sems = refs[25:]
+    units, _, wide = gate.shape
+    lead = 2
+    for low, high, sem in ((0, lead, 0), (lead, units, 1)):
+        fetch(order, ids, blocks, 3 * units, low, high, into_rows(gate, 0), sems.at[sem])
+        fetch(
+            order, ids, blocks, 3 * units, units + low, units + high,
+            into_rows(up, units), sems.at[sem],
+        )
+    fetch(order, ids, blocks, 3 * units, 2 * units, 3 * units, into_blocks(down, 2 * units), sems.at[2])
     rows = pieces[0].shape[0]
-    for k in range(count):
-        x_all[k * rows : (k + 1) * rows, :] = pieces[k][...]
-
-    @pl.loop(0, tiles)
-    def _(j):
-        pltpu.make_async_copy(first.at[j], first.at[j], sem_first.at[j]).wait()
-        both = jnp.dot(x_all[...], first[j], preferred_element_type=jnp.float32)
-        hidden[:, pl.ds(pl.multiple_of(j * unit, unit), unit)] = (
-            gelu(both[:, :unit]) * both[:, unit:]
-        ).astype(hidden.dtype)
-
-    @pl.loop(0, 8)
-    def _(n):
-        pltpu.make_async_copy(second.at[n], second.at[n], sem_second.at[n]).wait()
-        columns = pl.ds(pl.multiple_of(n * block, block), block)
-        part = jnp.dot(hidden[...], second[n], preferred_element_type=jnp.float32).astype(
-            outs[0].dtype
-        )
-        for k in range(count):
-            outs[k][:, columns] = part[k * rows : (k + 1) * rows, :]
+    for k, piece in enumerate((6, 7, 4, 5, 2, 3, 0, 1)):
+        x_all[k * rows : (k + 1) * rows, :] = pieces[piece][...]
+    for j in range(units):
+        if j in (0, lead):
+            part = pl.ds(j, lead if j == 0 else units - lead)
+            arrived(gate.at[part], sems.at[j // lead])
+            arrived(up.at[part], sems.at[j // lead])
+        gated = jnp.dot(x_all[...], gate[j], preferred_element_type=jnp.float32)
+        upped = jnp.dot(x_all[...], up[j], preferred_element_type=jnp.float32)
+        hidden[:, j * wide : (j + 1) * wide] = (gelu(gated) * upped).astype(hidden.dtype)
+    arrived(down, sems.at[2])
+    for n in range(8):
+        part = jnp.dot(
+            hidden[...], down[n].reshape(units * wide, wide), preferred_element_type=jnp.float32
+        ).astype(outs[0].dtype)
+        for k in range(6):
+            outs[k][:, n * wide : (n + 1) * wide] = part[k * rows : (k + 1) * rows, :]
+        outs[6][:, n * wide : (n + 1) * wide] = part[6 * rows :, :]
 
 
 def residual(base, shares, half):
@@ -512,12 +506,12 @@
 
 
 def plane_gather_split(block):
-    half = block.shape[0] // 2
+    cut = (block.shape[0] + 1) // 2
     held = {0: block}
     for mask in (2, 4, 1):
         held[mask] = exchange(block, mask)
-    low = exchange(held[4][:half], 2)
-    high = exchange(held[2][half:], 4)
+    low = exchange(held[4][:cut], 2)
+    high = exchange(held[2][cut:], 4)
     for mask in (3, 5):
         held[mask] = exchange(held[mask ^ 1], 1)
     pairs = [exchange(low, 1), exchange(high, 1)]
@@ -580,7 +574,7 @@
 
     qkv_own = call(
         pack_kernel, [], [w_query, w_key, w_value], [],
-        shape((block, 3 * inner), bf16), [], 2 * block * inner, 12 * block * inner,
+        shape((3 * inner // block, block, block), bf16), [], 2 * block * inner, 12 * block * inner,
     )
     low, high = call(
         rms_kernel, [], [hidden_states, gain_attn.reshape(1, width)], [],
@@ -591,18 +585,17 @@
     out_blocks = plane_gather(w_out)
     feed_own = call(
         pack_kernel, [], [w_gate, w_up, w_down], [],
-        shape((block, 3 * hidden), bf16), [], 2 * block * hidden, 12 * block * hidden,
+        shape((3 * hidden // block, block, block), bf16), [], 2 * block * hidden, 12 * block * hidden,
     )
     feed = plane_gather_split(feed_own)
 
-    tile = 2 * TILE
     projected = call(
         project_kernel, [shard_order, ids], normed, qkv,
         shape((length_all, 3 * inner), bf16),
         [
             pltpu.VMEM((length_all, width), bf16),
-            pltpu.VMEM((3 * inner // tile, width, tile), bf16),
-            pltpu.SemaphoreType.DMA((3 * inner // tile,)),
+            pltpu.VMEM((3 * inner // block, width, block), bf16),
+            pltpu.SemaphoreType.DMA((3,)),
         ],
         6 * length_all * width * inner, 6 * width * inner,
     )
@@ -633,26 +626,20 @@
     )
     normed = half_gather(low, high)
 
-    def feed_forward(pieces):
-        count = len(pieces)
-        return call(
-            functools.partial(feed_kernel, count), [shard_order, ids], pieces, feed,
-            [half_bf] * count,
-            [
-                pltpu.VMEM((count * half, width), bf16),
-                pltpu.VMEM((count * half, hidden), bf16),
-                pltpu.VMEM((hidden // tile, width, 2 * tile), bf16),
-                pltpu.VMEM((8, hidden, block), bf16),
-                pltpu.SemaphoreType.DMA((hidden // tile,)),
-                pltpu.SemaphoreType.DMA((8,)),
-            ],
-            6 * count * half * width * hidden, 6 * width * hidden,
-        )
-
-    near = feed_forward(normed[:6])
-    far = feed_forward(normed[6:])
-    own = jnp.concatenate(near[:2])
-    shares = half_scatter(far[0], far[1], near[4], near[5], near[2], near[3], own)
+    units = hidden // block
+    parts = call(
+        feed_kernel, [shard_order, ids], normed, feed, [half_bf] * 6 + [row_bf],
+        [
+            pltpu.VMEM((length_all, width), bf16),
+            pltpu.VMEM((length_all, hidden), bf16),
+            pltpu.VMEM((units, width, block), bf16),
+            pltpu.VMEM((units, width, block), bf16),
+            pltpu.VMEM((8, units, block, block), bf16),
+            pltpu.SemaphoreType.DMA((3,)),
+        ],
+        6 * length_all * width * hidden, 6 * width * hidden,
+    )
+    shares = half_scatter(*parts)
     output_rows, pool = call(
         final_kernel, [lengths, ids],
         [mid, *shares, gain_final.reshape(1, width), w_reward.reshape(1, width)], [],

time: 278 us -> 272 us (0.978)
  waiting for transfers between devices: 130 us -> 146 us
  Pallas kernels: 67.9 us -> 54.5 us
  starting transfers between devices: 55.8 us -> 49.6 us
    ppermute x24, waiting for transfers between devices: 90.2 us -> 118 us  [shift_rows(): return lax.ppermute(block, 'tensor', ring_pairs(step))]
    ppermute x24, starting transfers between devices: 40.2 us -> 28.2 us  [shift_rows(): return lax.ppermute(block, 'tensor', ring_pairs(step))]
    ppermute x28, waiting for transfers between devices: 33.3 us -> 22.1 us  [exchange(): return lax.ppermute(block, 'dp', [(i, i ^ mask) for i in range(8)])]
    pallas_call x9 -> x8, Pallas kernels: 54.4 us -> 43.4 us  [call(): pl.pallas_call(kernel, out_shape=out_list, grid_spec=pltpu.PrefetchScalar...]
    ppermute x28, starting transfers between devices: 14 us -> 18.9 us  [exchange(): return lax.ppermute(block, 'dp', [(i, i ^ mask) for i in range(8)])]
  transfers between devices with their start and end apart: 54 -> 54, of which waited for: 27 -> 30; matrix products, arithmetic and copies ran while one was open for 5% -> 4% of each run, Pallas kernels for 23% -> 13%
where the time goes in v1:
time: 272 us; the launch traced here: 271 us
  waiting for transfers between devices  146 us (54%)
  Pallas kernels  54.5 us (20%)
  starting transfers between devices  49.6 us (18%)
  local copies, waits for them, and re-layouts  9.86 us (4%)
  between operations  6.04 us (2%)
  other arithmetic  5.47 us (2%)
    ppermute x24, waiting for transfers between devices, shift_rows(): return lax.ppermute(block, 'tensor', ring_pairs(step))  118 us
    pallas_call x8, Pallas kernels, call(): pl.pallas_call(kernel, out_shape=out_list, grid_spec=pltpu.PrefetchScalar...  43.4 us
    ppermute x24, starting transfers between devices, shift_rows(): return lax.ppermute(block, 'tensor', ring_pairs(step))  28.2 us
    ppermute x28, waiting for transfers between devices, exchange(): return lax.ppermute(block, 'dp', [(i, i ^ mask) for i in range(8)])  22.1 us
    ppermute x28, starting transfers between devices, exchange(): return lax.ppermute(block, 'dp', [(i, i ^ mask) for i in range(8)])  18.9 us
    pallas_call x1, Pallas kernels, attention(): pl.pallas_call(attention_kernel, out_shape=jax.ShapeDtypeStruct((span, in...  11.1 us
    ppermute x2, waiting for transfers between devices, layer(): lax.ppermute(total, 'tensor', [(i, i ^ step) for i in range(4)])  5.81 us
  transfers between devices with their start and end apart: 54, of which 30 were waited for; matrix products, arithmetic and copies ran while one was open for 4% of the time, Pallas kernels for 13%

profile of v1, /device:TPU:0, one launch (start us, length us, event | category | flops | bytes accessed | tf_op | source)
XLA Modules:
  0.0 271.4 jit_solution(3617704237811815228)
XLA Ops:
  17.5 4.9 %collective-permute-done.1.refs_3_ = bf16[64,2048]{1,0:T(8,128)(2,1)} collective-permute-done((bf16[64,2048]{1,0:T(8,128)(2,1)}, bf16[64,2048]{1,0:T(8,128)(2,1)}, u32[]{:S(2)}, u32[]{:S(2)}) %collective-permute-start.1) | collective-permute-done | bytes 262176 | tf_op jit(solution)/shard_map/ppermute | solution.py:492
  22.3 3.6 %collective-permute-done.2.refs_4_ = bf16[64,2048]{1,0:T(8,128)(2,1)S(1)} collective-permute-done((bf16[64,2048]{1,0:T(8,128)(2,1)}, bf16[64,2048]{1,0:T(8,128)(2,1)S(1)}, u32[]{:S(2)}, u32[]{:S(2)}) %collective-permute-start.2) | collective-permute-done | bytes 262176 | tf_op jit(solution)/shard_map/ppermute | solution.py:492
  27.3 4.0 %collective-permute-done.3.refs_5_ = bf16[64,2048]{1,0:T(8,128)(2,1)S(1)} collective-permute-done((bf16[64,2048]{1,0:T(8,128)(2,1)}, bf16[64,2048]{1,0:T(8,128)(2,1)S(1)}, u32[]{:S(2)}, u32[]{:S(2)}) %collective-permute-start.3) | collective-permute-done | bytes 262176 | tf_op jit(solution)/shard_map/ppermute | solution.py:492
  36.5 8.8 %collective-permute-done.18.refs_4_ = bf16[512,256]{1,0:T(8,128)(2,1)} collective-permute-done((bf16[512,256]{1,0:T(8,128)(2,1)S(1)}, bf16[512,256]{1,0:T(8,128)(2,1)}, u32[]{:S(2)}, u32[]{:S(2)}) %collective-permute-start.18) | collective-permute-done | bytes 262176 | tf_op jit(solution)/shard_map/ppermute | solution.py:496
  51.0 5.5 %collective-permute-done.4.refs_6_ = bf16[64,2048]{1,0:T(8,128)(2,1)S(1)} collective-permute-done((bf16[64,2048]{1,0:T(8,128)(2,1)}, bf16[64,2048]{1,0:T(8,128)(2,1)S(1)}, u32[]{:S(2)}, u32[]{:S(2)}) %collective-permute-start.4) | collective-permute-done | bytes 262176 | tf_op jit(solution)/shard_map/ppermute | solution.py:492
  73.4 8.6 %shard_map.160.q_ref.k_ref.v_ref = bf16[512,1536]{1,0:T(8,128)(2,1)} custom-call(s32[8]{0:T(128)} %order.5, s32[2]{0:T(128)} %pad_add_fusion.ids, bf16[64,2048]{1,0:T(8,128)(2,1)} %get-tuple-element.23.refs_0_, bf16[64,2048]{1,0:T(8,128)(2,1)} %get-tuple-element.24.refs_1_, bf16[64,2048]{1,0:T(8,128)(2,1)} %collective-permute-done.refs_2_, ...), custom_call_target="tpu_custom_call" | custom-call | flops 3221225472 | bytes 6291456 | tf_op jit(solution)/shard_map/pallas_call | solution.py:475
  82.6 11.1 %attention.1.context = bf16[512,512]{1,0:T(8,128)(2,1)} custom-call(s32[1]{0:T(128)S(6)} %copy.17.length_ref.length, bf16[512,1536]{1,0:T(8,128)(2,1)} %shard_map.160.q_ref.k_ref.v_ref, bf16[512,1536]{1,0:T(8,128)(2,1)} %shard_map.160.q_ref.k_ref.v_ref, bf16[512,1536]{1,0:T(8,128)(2,1)} %shard_map.160.q_ref.k_ref.v_ref, f32[4,2,512]{2,1,0:T(2,128)} %reshape.65.bias_ref), custom_call_target="tpu_custom_call" | custom-call | flops 2147483648 | bytes 2097152 | tf_op jit(solution)/shard_map/attention/pallas_call | solution.py:155
  95.1 6.7 %shard_map.161 = (bf16[64,2048]{1,0:T(8,128)(2,1)}, bf16[64,2048]{1,0:T(8,128)(2,1)}, bf16[64,2048]{1,0:T(8,128)(2,1)}, bf16[64,2048]{1,0:T(8,128)(2,1)}, bf16[6...) custom-call(s32[8]{0:T(128)} %order.5, s32[2]{0:T(128)} %pad_add_fusion.ids, ...), custom_call_target="tpu_custom_call" | custom-call | flops 1073741824 | bytes 2097152 | tf_op jit(solution)/shard_map/pallas_call | solution.py:475
  101.9 11.2 %collective-permute-done.22 = bf16[64,2048]{1,0:T(8,128)(2,1)S(1)} collective-permute-done((bf16[64,2048]{1,0:T(8,128)(2,1)}, bf16[64,2048]{1,0:T(8,128)(2,1)S(1)}, u32[]{:S(2)}, u32[]{:S(2)}) %collective-permute-start.22) | collective-permute-done | bytes 262176 | tf_op jit(solution)/shard_map/ppermute | solution.py:492
  114.1 4.6 %collective-permute-done.24.refs_2_ = bf16[64,2048]{1,0:T(8,128)(2,1)S(1)} collective-permute-done((bf16[64,2048]{1,0:T(8,128)(2,1)}, bf16[64,2048]{1,0:T(8,128)(2,1)S(1)}, u32[]{:S(2)}, u32[]{:S(2)}) %collective-permute-start.24) | collective-permute-done | bytes 262176 | tf_op jit(solution)/shard_map/ppermute | solution.py:492
  118.7 4.7 %collective-permute-done.26 = bf16[64,2048]{1,0:T(8,128)(2,1)S(1)} collective-permute-done((bf16[64,2048]{1,0:T(8,128)(2,1)}, bf16[64,2048]{1,0:T(8,128)(2,1)S(1)}, u32[]{:S(2)}, u32[]{:S(2)}) %collective-permute-start.26) | collective-permute-done | bytes 262176 | tf_op jit(solution)/shard_map/ppermute | solution.py:492
  125.0 3.4 %collective-permute-start.27 = (bf16[64,2048]{1,0:T(8,128)(2,1)S(1)}, bf16[64,2048]{1,0:T(8,128)(2,1)S(1)}, u32[]{:S(2)}, u32[]{:S(2)}) collective-permute-start(bf16[64,2048]{1,0:T(8,128)(2,1)S(1)} %add_convert_fusion.2), channel_id=1, source_target_pairs={{0,3},{1,0},{2,1},{3,2},{4,7},{5,4},{6,5},{7,6},{8,11},{9,8},{10,9... | collective-permute-start | bytes 786440 | tf_op jit(solution)/shard_map/ppermute | solution.py:492
  129.7 4.1 %collective-permute-done.25.refs_3_ = bf16[64,2048]{1,0:T(8,128)(2,1)S(1)} collective-permute-done((bf16[64,2048]{1,0:T(8,128)(2,1)}, bf16[64,2048]{1,0:T(8,128)(2,1)S(1)}, u32[]{:S(2)}, u32[]{:S(2)}) %collective-permute-start.25) | collective-permute-done | bytes 262176 | tf_op jit(solution)/shard_map/ppermute | solution.py:492
  144.5 9.9 %collective-permute-done.28.refs_2_ = bf16[64,2048]{1,0:T(8,128)(2,1)S(1)} collective-permute-done((bf16[64,2048]{1,0:T(8,128)(2,1)}, bf16[64,2048]{1,0:T(8,128)(2,1)S(1)}, u32[]{:S(2)}, u32[]{:S(2)}) %collective-permute-start.28) | collective-permute-done | bytes 262176 | tf_op jit(solution)/shard_map/ppermute | solution.py:492
  154.4 10.4 %collective-permute-done.29.refs_3_ = bf16[64,2048]{1,0:T(8,128)(2,1)S(1)} collective-permute-done((bf16[64,2048]{1,0:T(8,128)(2,1)}, bf16[64,2048]{1,0:T(8,128)(2,1)S(1)}, u32[]{:S(2)}, u32[]{:S(2)}) %collective-permute-start.29) | collective-permute-done | bytes 262176 | tf_op jit(solution)/shard_map/ppermute | solution.py:492
  165.3 6.8 %collective-permute-done.30.refs_4_ = bf16[64,2048]{1,0:T(8,128)(2,1)S(1)} collective-permute-done((bf16[64,2048]{1,0:T(8,128)(2,1)}, bf16[64,2048]{1,0:T(8,128)(2,1)S(1)}, u32[]{:S(2)}, u32[]{:S(2)}) %collective-permute-start.30) | collective-permute-done | bytes 262176 | tf_op jit(solution)/shard_map/ppermute | solution.py:492
  173.1 8.4 %collective-permute-done.31.refs_5_ = bf16[64,2048]{1,0:T(8,128)(2,1)S(1)} collective-permute-done((bf16[64,2048]{1,0:T(8,128)(2,1)}, bf16[64,2048]{1,0:T(8,128)(2,1)S(1)}, u32[]{:S(2)}, u32[]{:S(2)}) %collective-permute-start.31) | collective-permute-done | bytes 262176 | tf_op jit(solution)/shard_map/ppermute | solution.py:492
  181.5 9.5 %collective-permute-done.32.refs_6_ = bf16[64,2048]{1,0:T(8,128)(2,1)S(1)} collective-permute-done((bf16[64,2048]{1,0:T(8,128)(2,1)S(1)}, bf16[64,2048]{1,0:T(8,128)(2,1)S(1)}, u32[]{:S(2)}, u32[]{:S(2)}) %collective-permute-start.32) | collective-permute-done | bytes 262176 | tf_op jit(solution)/shard_map/ppermute | solution.py:492
  193.6 3.9 %collective-permute-done.33.refs_7_ = bf16[64,2048]{1,0:T(8,128)(2,1)S(1)} collective-permute-done((bf16[64,2048]{1,0:T(8,128)(2,1)S(1)}, bf16[64,2048]{1,0:T(8,128)(2,1)S(1)}, u32[]{:S(2)}, u32[]{:S(2)}) %collective-permute-start.33) | collective-permute-done | bytes 262176 | tf_op jit(solution)/shard_map/ppermute | solution.py:492
  199.4 14.3 %shard_map.164 = (bf16[64,2048]{1,0:T(8,128)(2,1)}, bf16[64,2048]{1,0:T(8,128)(2,1)}, bf16[64,2048]{1,0:T(8,128)(2,1)}, bf16[64,2048]{1,0:T(8,128)(2,1)}, bf16[6...) custom-call(s32[8]{0:T(128)} %order.5, s32[2]{0:T(128)} %pad_add_fusion.ids, ...), custom_call_target="tpu_custom_call" | custom-call | flops 8053063680 | bytes 15728640 | tf_op jit(solution)/shard_map/pallas_call | solution.py:475
  220.2 5.4 %collective-permute-done.43 = bf16[64,2048]{1,0:T(8,128)(2,1)S(1)} collective-permute-done((bf16[64,2048]{1,0:T(8,128)(2,1)}, bf16[64,2048]{1,0:T(8,128)(2,1)S(1)}, u32[]{:S(2)}, u32[]{:S(2)}) %collective-permute-start.43) | collective-permute-done | bytes 262176 | tf_op jit(solution)/shard_map/ppermute | solution.py:492
  226.6 10.6 %collective-permute-done.47 = bf16[64,2048]{1,0:T(8,128)(2,1)S(1)} collective-permute-done((bf16[64,2048]{1,0:T(8,128)(2,1)}, bf16[64,2048]{1,0:T(8,128)(2,1)S(1)}, u32[]{:S(2)}, u32[]{:S(2)}) %collective-permute-start.47) | collective-permute-done | bytes 262176 | tf_op jit(solution)/shard_map/ppermute | solution.py:492
  240.8 3.9 %collective-permute-done.48.refs_4_ = bf16[64,2048]{1,0:T(8,128)(2,1)S(1)} collective-permute-done((bf16[64,2048]{1,0:T(8,128)(2,1)S(1)}, bf16[64,2048]{1,0:T(8,128)(2,1)S(1)}, u32[]{:S(2)}, u32[]{:S(2)}) %collective-permute-start.48) | collective-permute-done | bytes 262176 | tf_op jit(solution)/shard_map/ppermute | solution.py:492
  245.4 3.6 %shard_map.165 = (f32[128,2048]{1,0:T(8,128)}, f32[8,128]{1,0:T(8,128)}) custom-call(s32[1]{0:T(128)S(6)} %copy.17.length_ref.length, s32[2]{0:T(128)} %pad_add_fusion.ids, f32[128,2048]{1,0:T(8,128)} %get-tuple-element.32.x_ref, bf16[128,2048]{1,0:T(8,128)(2,1)} %get-tuple-element.35.refs_0_, bf16[64,2048]{1,0:T(8,128)(2,1)} %copy-done.8, ...), custom_call_target="tpu_custom_call" | custom-call | flops 2097152 | bytes 4194304 | tf_op jit(solution)/shard_map/pallas_call | solution.py:475
  (175 shorter events, 97.5 us)
Async XLA Ops:
  8.0 38.1 %collective-permute-start.7 = (bf16[6,256,256]{2,1,0:T(8,128)(2,1)}, bf16[6,256,256]{2,1,0:T(8,128)(2,1)S(1)}, u32[]{:S(2)}, u32[]{:S(2)}) collective-permute-start(bf16[6,256,256]{2,1,0:T(8,128)(2,1)} %shard_map.159.refs_8_), channel_id=1, source_target_pairs={{0,8},{4,12},{8,0},{12,4},{16,24},{20,28},{24,16},{28,20},{1,9},{5... | collective-permute-start | bytes 2359304 | tf_op jit(solution)/shard_map/ppermute | solution.py:496
  9.5 39.6 %collective-permute-start.9 = (bf16[6,256,256]{2,1,0:T(8,128)(2,1)}, bf16[6,256,256]{2,1,0:T(8,128)(2,1)S(1)}, u32[]{:S(2)}, u32[]{:S(2)}) collective-permute-start(bf16[6,256,256]{2,1,0:T(8,128)(2,1)} %shard_map.159.refs_8_), channel_id=1, source_target_pairs={{0,16},{4,20},{8,24},{12,28},{16,0},{20,4},{24,8},{28,12},{1,17},{... | collective-permute-start | bytes 2359304 | tf_op jit(solution)/shard_map/ppermute | solution.py:496
  14.8 16.5 %collective-permute-start.3 = (bf16[64,2048]{1,0:T(8,128)(2,1)}, bf16[64,2048]{1,0:T(8,128)(2,1)S(1)}, u32[]{:S(2)}, u32[]{:S(2)}) collective-permute-start(bf16[64,2048]{1,0:T(8,128)(2,1)} %get-tuple-element.24.refs_1_), channel_id=1, source_target_pairs={{0,3},{1,0},{2,1},{3,2},{4,7},{5,4},{6,5},{7,6},{8,11},{9,8},{10,9... | collective-permute-start | bytes 786440 | tf_op jit(solution)/shard_map/ppermute | solution.py:492
  32.9 34.4 %collective-permute-start.6 = (bf16[6,256,256]{2,1,0:T(8,128)(2,1)}, bf16[6,256,256]{2,1,0:T(8,128)(2,1)S(1)}, u32[]{:S(2)}, u32[]{:S(2)}) collective-permute-start(bf16[6,256,256]{2,1,0:T(8,128)(2,1)} %shard_map.159.refs_8_), channel_id=1, source_target_pairs={{0,4},{4,0},{8,12},{12,8},{16,20},{20,16},{24,28},{28,24},{1,5},{5... | collective-permute-start | bytes 2359304 | tf_op jit(solution)/shard_map/ppermute | solution.py:496
  34.0 15.3 %collective-permute-start.20 = (bf16[512,256]{1,0:T(8,128)(2,1)S(1)}, bf16[512,256]{1,0:T(8,128)(2,1)}, u32[]{:S(2)}, u32[]{:S(2)}) collective-permute-start(bf16[512,256]{1,0:T(8,128)(2,1)S(1)} %copy-done.16), channel_id=1, source_target_pairs={{0,24},{4,28},{8,16},{12,20},{16,8},{20,12},{24,0},{28,4},{1,25},{... | collective-permute-start | bytes 786440 | tf_op jit(solution)/shard_map/ppermute | solution.py:496
  49.1 20.2 %collective-permute-start.8 = (bf16[6,256,256]{2,1,0:T(8,128)(2,1)S(1)}, bf16[6,256,256]{2,1,0:T(8,128)(2,1)S(1)}, u32[]{:S(2)}, u32[]{:S(2)}) collective-permute-start(bf16[6,256,256]{2,1,0:T(8,128)(2,1)S(1)} %collective-permute-done.7.refs_10_), channel_id=1, source_target_pairs={{0,4},{4,0},{8,12},{12,8},{16,20},{20,16},{24,28},{28,24},{1,5},{5... | collective-permute-start | bytes 2359304 | tf_op jit(solution)/shard_map/ppermute | solution.py:496
  67.3 57.7 %collective-permute-start.37 = (bf16[15,256,256]{2,1,0:T(8,128)(2,1)}, bf16[15,256,256]{2,1,0:T(8,128)(2,1)}, u32[]{:S(2)}, u32[]{:S(2)}) collective-permute-start(bf16[15,256,256]{2,1,0:T(8,128)(2,1)} %shard_map.163.refs_8_), channel_id=1, source_target_pairs={{0,16},{4,20},{8,24},{12,28},{16,0},{20,4},{24,8},{28,12},{1,17},{... | collective-permute-start | bytes 5898248 | tf_op jit(solution)/shard_map/ppermute | solution.py:496
  69.4 65.2 %collective-permute-start.35 = (bf16[15,256,256]{2,1,0:T(8,128)(2,1)}, bf16[15,256,256]{2,1,0:T(8,128)(2,1)}, u32[]{:S(2)}, u32[]{:S(2)}) collective-permute-start(bf16[15,256,256]{2,1,0:T(8,128)(2,1)} %shard_map.163.refs_8_), channel_id=1, source_target_pairs={{0,8},{4,12},{8,0},{12,4},{16,24},{20,28},{24,16},{28,20},{1,9},{5... | collective-permute-start | bytes 5898248 | tf_op jit(solution)/shard_map/ppermute | solution.py:496
  72.8 20.8 %collective-permute-start.19 = (bf16[512,256]{1,0:T(8,128)(2,1)}, bf16[512,256]{1,0:T(8,128)(2,1)S(1)}, u32[]{:S(2)}, u32[]{:S(2)}) collective-permute-start(bf16[512,256]{1,0:T(8,128)(2,1)} %collective-permute-done.18.refs_4_), channel_id=1, source_target_pairs={{0,4},{4,0},{8,12},{12,8},{16,20},{20,16},{24,28},{28,24},{1,5},{5... | collective-permute-start | bytes 786440 | tf_op jit(solution)/shard_map/ppermute | solution.py:496
  73.3 20.3 %collective-permute-start.21 = (bf16[512,256]{1,0:T(8,128)(2,1)}, bf16[512,256]{1,0:T(8,128)(2,1)S(1)}, u32[]{:S(2)}, u32[]{:S(2)}) collective-permute-start(bf16[512,256]{1,0:T(8,128)(2,1)} %collective-permute-done.20.refs_6_), channel_id=1, source_target_pairs={{0,4},{4,0},{8,12},{12,8},{16,20},{20,16},{24,28},{28,24},{1,5},{5... | collective-permute-start | bytes 786440 | tf_op jit(solution)/shard_map/ppermute | solution.py:496
  82.1 62.0 %collective-permute-start.34 = (bf16[15,256,256]{2,1,0:T(8,128)(2,1)S(1)}, bf16[15,256,256]{2,1,0:T(8,128)(2,1)}, u32[]{:S(2)}, u32[]{:S(2)}) collective-permute-start(bf16[15,256,256]{2,1,0:T(8,128)(2,1)S(1)} %copy-done.1), channel_id=1, source_target_pairs={{0,4},{4,0},{8,12},{12,8},{16,20},{20,16},{24,28},{28,24},{1,5},{5... | collective-permute-start | bytes 5898248 | tf_op jit(solution)/shard_map/ppermute | solution.py:496
  101.8 16.9 %collective-permute-start.24 = (bf16[64,2048]{1,0:T(8,128)(2,1)}, bf16[64,2048]{1,0:T(8,128)(2,1)S(1)}, u32[]{:S(2)}, u32[]{:S(2)}) collective-permute-start(bf16[64,2048]{1,0:T(8,128)(2,1)} %get-tuple-element.28), channel_id=1, source_target_pairs={{0,1},{1,2},{2,3},{3,0},{4,5},{5,6},{6,7},{7,4},{8,9},{9,10},{10,1... | collective-permute-start | bytes 786440 | tf_op jit(solution)/shard_map/ppermute | solution.py:492
  118.7 15.1 %collective-permute-start.25 = (bf16[64,2048]{1,0:T(8,128)(2,1)}, bf16[64,2048]{1,0:T(8,128)(2,1)S(1)}, u32[]{:S(2)}, u32[]{:S(2)}) collective-permute-start(bf16[64,2048]{1,0:T(8,128)(2,1)} %get-tuple-element.29), channel_id=1, source_target_pairs={{0,3},{1,0},{2,1},{3,2},{4,7},{5,4},{6,5},{7,6},{8,11},{9,8},{10,9... | collective-permute-start | bytes 786440 | tf_op jit(solution)/shard_map/ppermute | solution.py:492
  125.0 15.3 %collective-permute-start.27 = (bf16[64,2048]{1,0:T(8,128)(2,1)S(1)}, bf16[64,2048]{1,0:T(8,128)(2,1)S(1)}, u32[]{:S(2)}, u32[]{:S(2)}) collective-permute-start(bf16[64,2048]{1,0:T(8,128)(2,1)S(1)} %add_convert_fusion.2), channel_id=1, source_target_pairs={{0,3},{1,0},{2,1},{3,2},{4,7},{5,4},{6,5},{7,6},{8,11},{9,8},{10,9... | collective-permute-start | bytes 786440 | tf_op jit(solution)/shard_map/ppermute | solution.py:492
  133.8 31.0 %collective-permute-start.39 = (bf16[8,256,256]{2,1,0:T(8,128)(2,1)S(1)}, bf16[8,256,256]{2,1,0:T(8,128)(2,1)}, u32[]{:S(2)}, u32[]{:S(2)}) collective-permute-start(bf16[8,256,256]{2,1,0:T(8,128)(2,1)S(1)} %slice.30), channel_id=1, source_target_pairs={{0,8},{4,12},{8,0},{12,4},{16,24},{20,28},{24,16},{28,20},{1,9},{5... | collective-permute-start | bytes 3145736 | tf_op jit(solution)/shard_map/ppermute | solution.py:496
  134.5 62.9 %collective-permute-start.36 = (bf16[15,256,256]{2,1,0:T(8,128)(2,1)}, bf16[15,256,256]{2,1,0:T(8,128)(2,1)}, u32[]{:S(2)}, u32[]{:S(2)}) collective-permute-start(bf16[15,256,256]{2,1,0:T(8,128)(2,1)} %collective-permute-done.35.refs_10_), channel_id=1, source_target_pairs={{0,4},{4,0},{8,12},{12,8},{16,20},{20,16},{24,28},{28,24},{1,5},{5... | collective-permute-start | bytes 5898248 | tf_op jit(solution)/shard_map/ppermute | solution.py:496
  135.6 61.9 %collective-permute-start.38 = (bf16[15,256,256]{2,1,0:T(8,128)(2,1)}, bf16[15,256,256]{2,1,0:T(8,128)(2,1)}, u32[]{:S(2)}, u32[]{:S(2)}) collective-permute-start(bf16[15,256,256]{2,1,0:T(8,128)(2,1)} %collective-permute-done.37.refs_12_), channel_id=1, source_target_pairs={{0,4},{4,0},{8,12},{12,8},{16,20},{20,16},{24,28},{28,24},{1,5},{5... | collective-permute-start | bytes 5898248 | tf_op jit(solution)/shard_map/ppermute | solution.py:496
  140.2 24.6 %collective-permute-start.40 = (bf16[7,256,256]{2,1,0:T(8,128)(2,1)}, bf16[7,256,256]{2,1,0:T(8,128)(2,1)}, u32[]{:S(2)}, u32[]{:S(2)}) collective-permute-start(bf16[7,256,256]{2,1,0:T(8,128)(2,1)} %slice.31), channel_id=1, source_target_pairs={{0,16},{4,20},{8,24},{12,28},{16,0},{20,4},{24,8},{28,12},{1,17},{... | collective-permute-start | bytes 2752520 | tf_op jit(solution)/shard_map/ppermute | solution.py:496
  164.7 32.8 %collective-permute-start.41 = (bf16[8,256,256]{2,1,0:T(8,128)(2,1)}, bf16[8,256,256]{2,1,0:T(8,128)(2,1)S(1)}, u32[]{:S(2)}, u32[]{:S(2)}) collective-permute-start(bf16[8,256,256]{2,1,0:T(8,128)(2,1)} %collective-permute-done.39.refs_14_), channel_id=1, source_target_pairs={{0,4},{4,0},{8,12},{12,8},{16,20},{20,16},{24,28},{28,24},{1,5},{5... | collective-permute-start | bytes 3145736 | tf_op jit(solution)/shard_map/ppermute | solution.py:496
  164.8 32.7 %collective-permute-start.42 = (bf16[7,256,256]{2,1,0:T(8,128)(2,1)}, bf16[7,256,256]{2,1,0:T(8,128)(2,1)S(1)}, u32[]{:S(2)}, u32[]{:S(2)}) collective-permute-start(bf16[7,256,256]{2,1,0:T(8,128)(2,1)} %collective-permute-done.40.refs_15_), channel_id=1, source_target_pairs={{0,4},{4,0},{8,12},{12,8},{16,20},{20,16},{24,28},{28,24},{1,5},{5... | collective-permute-start | bytes 2752520 | tf_op jit(solution)/shard_map/ppermute | solution.py:496
  213.8 24.9 %collective-permute-start.45 = (bf16[64,2048]{1,0:T(8,128)(2,1)}, bf16[64,2048]{1,0:T(8,128)(2,1)S(1)}, u32[]{:S(2)}, u32[]{:S(2)}) collective-permute-start(bf16[64,2048]{1,0:T(8,128)(2,1)} %get-tuple-element.38), channel_id=1, source_target_pairs={{0,1},{1,2},{2,3},{3,0},{4,5},{5,6},{6,7},{7,4},{8,9},{9,10},{10,1... | collective-permute-start | bytes 786440 | tf_op jit(solution)/shard_map/ppermute | solution.py:492
  215.4 23.3 %collective-permute-start.46 = (bf16[64,2048]{1,0:T(8,128)(2,1)}, bf16[64,2048]{1,0:T(8,128)(2,1)S(1)}, u32[]{:S(2)}, u32[]{:S(2)}) collective-permute-start(bf16[64,2048]{1,0:T(8,128)(2,1)} %get-tuple-element.39), channel_id=1, source_target_pairs={{0,3},{1,0},{2,1},{3,2},{4,7},{5,4},{6,5},{7,6},{8,11},{9,8},{10,9... | collective-permute-start | bytes 786440 | tf_op jit(solution)/shard_map/ppermute | solution.py:492
  218.2 19.1 %collective-permute-start.47 = (bf16[64,2048]{1,0:T(8,128)(2,1)}, bf16[64,2048]{1,0:T(8,128)(2,1)S(1)}, u32[]{:S(2)}, u32[]{:S(2)}) collective-permute-start(bf16[64,2048]{1,0:T(8,128)(2,1)} %get-tuple-element.41), channel_id=1, source_target_pairs={{0,3},{1,0},{2,1},{3,2},{4,7},{5,4},{6,5},{7,6},{8,11},{9,8},{10,9... | collective-permute-start | bytes 786440 | tf_op jit(solution)/shard_map/ppermute | solution.py:492
  226.6 14.2 %collective-permute-start.44 = (bf16[64,2048]{1,0:T(8,128)(2,1)S(1)}, bf16[64,2048]{1,0:T(8,128)(2,1)S(1)}, u32[]{:S(2)}, u32[]{:S(2)}) collective-permute-start(bf16[64,2048]{1,0:T(8,128)(2,1)S(1)} %add_convert_fusion.1), channel_id=1, source_target_pairs={{0,1},{1,2},{2,3},{3,0},{4,5},{5,6},{6,7},{7,4},{8,9},{9,10},{10,1... | collective-permute-start | bytes 786440 | tf_op jit(solution)/shard_map/ppermute | solution.py:492
  (61 other events, 698.9 us)

commit v2 on v1

--- a/solution.py
+++ b/solution.py
@@ -1,4 +1,5 @@
 import functools
+import math
 
 import jax
 import jax.numpy as jnp
@@ -10,6 +11,9 @@
 
 DK = 64
 TILE = 128
+GROUP = 512
+SPARE = 4 << 20
+
 
 bucket_edges = (12, 16, 23, 32, 46, 64, 91)
 
@@ -119,38 +123,54 @@
     one = jnp.ones_like(values)
     sums = []
     for head in range(2):
-        table = bias_ref[0, head : head + 1, :]
-        near = pltpu.roll(jnp.broadcast_to(table, (TILE, 4 * TILE)), 0, 1, stride=1, stride_axis=0)
+        table = bias_ref[pl.ds(2 * pl.program_id(0) + head, 1), :]
+        near = pltpu.roll(
+            jnp.broadcast_to(table, (TILE, 4 * TILE)), 0, 1, stride=1, stride_axis=0
+        )
         own = first if head == 0 else jnp.logical_not(first)
         with_ones = jnp.where(own, values, one)
         far_left, far_right = table[:, 1:2], table[:, 4 * TILE - 1 :]
         heads = []
-        for block in range(blocks):
-            queries = q_ref[block * TILE : (block + 1) * TILE, :]
+        for group in range(span // GROUP):
+            queries = q_ref[group * GROUP : (group + 1) * GROUP, :]
             queries = jnp.where(own, queries, jnp.zeros_like(queries))
-            scores = lax.dot_general(queries, keys, (((1,), (1,)), ((), ())), preferred_element_type=jnp.float32)
-            pieces = []
-            for other in range(blocks):
-                at = slice(other * TILE, (other + 1) * TILE)
-                delta = other - block
-                if abs(delta) > 1:
-                    bias = masked[:, at] + (far_left if delta < 0 else far_right)
-                    pieces.append(scores[:, at] + bias)
-                else:
-                    pieces.append(scores[:, at] + near[:, (delta + 2) * TILE : (delta + 3) * TILE] + masked[:, at])
-            top = jnp.max(functools.reduce(jnp.maximum, pieces), axis=-1, keepdims=True)
-            soft = jnp.concatenate([jnp.exp(p - top).astype(jnp.bfloat16) for p in pieces], axis=1)
-            heads.append(jnp.dot(soft, with_ones, preferred_element_type=jnp.float32))
+            scores = lax.dot_general(
+                queries, keys, (((1,), (1,)), ((), ())), preferred_element_type=jnp.float32
+            )
+            soft = []
+            for block in range(group * GROUP // TILE, (group + 1) * GROUP // TILE):
+                row = block * TILE - group * GROUP
+                pieces = []
+                for other in range(blocks):
+                    at = slice(other * TILE, (other + 1) * TILE)
+                    delta = other - block
+                    if abs(delta) > 1:
+                        bias = masked[:, at] + (far_left if delta < 0 else far_right)
+                    else:
+                        bias = near[:, (delta + 2) * TILE : (delta + 3) * TILE] + masked[:, at]
+                    pieces.append(scores[row : row + TILE, at] + bias)
+                top = jnp.max(functools.reduce(jnp.maximum, pieces), axis=-1, keepdims=True)
+                soft.append(
+                    jnp.concatenate(
+                        [jnp.exp(p - top).astype(jnp.bfloat16) for p in pieces], axis=1
+                    )
+                )
+            heads.append(
+                jnp.dot(
+                    jnp.concatenate(soft, axis=0), with_ones, preferred_element_type=jnp.float32
+                )
+            )
         sums.append(heads)
-    for block in range(blocks):
-        zero, last = sums[0][block], sums[1][block]
+    for group in range(span // GROUP):
+        zero, last = sums[0][group], sums[1][group]
         total = pltpu.roll(jnp.where(first, last, zero), DK, 1)
-        o_ref[block * TILE : (block + 1) * TILE, :] = (jnp.where(first, zero, last) / total).astype(o_ref.dtype)
-
-
-def attention(length, projected, bias_table):
-    span, width = projected.shape
-    inner = width // 3
+        o_ref[group * GROUP : (group + 1) * GROUP, :] = (
+            jnp.where(first, zero, last) / total
+        ).astype(o_ref.dtype)
+
+
+def attention(length, queries, keys, values, bias_table):
+    span, inner = queries.shape
     pairs = inner // (2 * DK)
     return pl.pallas_call(
         attention_kernel,
@@ -160,19 +180,20 @@
             grid=(pairs,),
             in_specs=[
                 pl.BlockSpec((span, 2 * DK), lambda p, n: (0, p)),
-                pl.BlockSpec((span, 2 * DK), lambda p, n: (0, pairs + p)),
-                pl.BlockSpec((span, 2 * DK), lambda p, n: (0, 2 * pairs + p)),
-                pl.BlockSpec((1, 2, 4 * TILE), lambda p, n: (p, 0, 0)),
+                pl.BlockSpec((span, 2 * DK), lambda p, n: (0, p)),
+                pl.BlockSpec((span, 2 * DK), lambda p, n: (0, p)),
+                pl.BlockSpec(bias_table.shape, lambda p, n: (0, 0)),
             ],
             out_specs=pl.BlockSpec((span, 2 * DK), lambda p, n: (0, p)),
         ),
         cost_estimate=pl.CostEstimate(
             flops=16 * span * span * inner,
-            bytes_accessed=2 * span * (width + inner),
+            bytes_accessed=8 * span * inner,
             transcendentals=span * span * inner // DK,
         ),
+        compiler_params=pltpu.CompilerParams(vmem_limit_bytes=10 << 20),
         name="attention",
-    )(length, projected, projected, projected, bias_table)
+    )(length, queries, keys, values, bias_table)
 
 
 def total_over(values_in, name):
@@ -229,16 +250,14 @@
     normed = ring_gather(rms_norm(own_rows, attn_gain).astype(jnp.bfloat16))
     projected = jnp.dot(normed, qkv_full, preferred_element_type=jnp.float32).astype(jnp.bfloat16)
 
-    heads = rel_bias.shape[1]
     relative = jnp.arange(4 * TILE, dtype=jnp.int32) - 2 * TILE
     onehot = (
         bucket_index(relative)[:, None]
         == jnp.arange(rel_bias.shape[0], dtype=jnp.int32)[None, :]
     ).astype(jnp.float32)
     bias_table = jnp.dot(onehot, rel_bias, precision=lax.Precision.HIGHEST).T
-    bias_table = bias_table.reshape(heads // 2, 2, 4 * TILE)
     length = lengths[0]
-    context = attention(lengths, projected, bias_table)
+    context = attention(lengths, *jnp.split(projected, 3, axis=1), bias_table)
 
     attn_partial = jnp.dot(context, out_full, preferred_element_type=jnp.float32).astype(
         jnp.bfloat16
@@ -315,30 +334,41 @@
     pltpu.make_async_copy(part, part, sem).wait()
 
 
-def rms_kernel(x_ref, gain_ref, low_ref, high_ref):
-    x = x_ref[...]
-    scale = lax.rsqrt(jnp.mean(x * x, axis=-1, keepdims=True) + 1e-06)
-    normed = (x * scale * gain_ref[...]).astype(jnp.bfloat16)
+def rms_kernel(gain_ref, x_hbm, low_ref, high_ref, x_ref, sems):
     half = low_ref.shape[0]
-    low_ref[...] = normed[:half]
-    high_ref[...] = normed[half:]
+    copies = [
+        pltpu.make_async_copy(
+            x_hbm.at[pl.ds(k * half, half)], x_ref.at[pl.ds(k * half, half)], sems.at[k]
+        )
+        for k in range(2)
+    ]
+    for copy in copies:
+        copy.start()
+    for k, out in enumerate((low_ref, high_ref)):
+        copies[k].wait()
+        x = x_ref[k * half : (k + 1) * half, :]
+        scale = lax.rsqrt(jnp.mean(x * x, axis=-1, keepdims=True) + 1e-06)
+        out[...] = (x * scale * gain_ref[...]).astype(jnp.bfloat16)
 
 
 def pack_kernel(*refs):
-    *sources, out = refs
+    *sources, out, sem = refs
     _, rows, wide = out.shape
     at = 0
     for s in sources:
         for i in range(s.shape[0] // rows):
             for j in range(s.shape[1] // wide):
-                out[at] = s[i * rows : (i + 1) * rows, j * wide : (j + 1) * wide]
+                pltpu.make_async_copy(
+                    s.at[pl.ds(i * rows, rows), pl.ds(j * wide, wide)], out.at[at], sem.at[0]
+                ).start()
                 at += 1
+    arrived(out, sem.at[0])
 
 
 def project_kernel(order, ids, *refs):
     pieces = refs[:8]
     blocks = refs[8:18]
-    out, x_all, w_all, sems = refs[18:]
+    *outs, x_all, w_all, sems = refs[18:]
     tiles, _, wide = w_all.shape
     stages = sems.shape[0]
     each = tiles // stages
@@ -354,7 +384,8 @@
     for j in range(tiles):
         if j % each == 0:
             arrived(w_all.at[pl.ds(j, each)], sems.at[j // each])
-        out[:, j * wide : (j + 1) * wide] = jnp.dot(
+        out, column = outs[j // each], (j % each) * wide
+        out[:, column : column + wide] = jnp.dot(
             x_all[...], w_all[j], preferred_element_type=jnp.float32
         ).astype(out.dtype)
 
@@ -363,19 +394,23 @@
     blocks = refs[:8]
     far_low, far_high, ahead_low, ahead_high, behind_low, behind_high, own = refs[8:15]
     x_all, w_all, sems = refs[15:]
+    wide = w_all.shape[2]
     for mask in range(8):
         where_to = true_block(order, ids, mask)
-        pltpu.make_async_copy(blocks[mask], w_all.at[where_to], sems.at[where_to]).start()
+        at = pl.multiple_of(lax.rem(where_to, 2) * (wide // 2), wide // 2)
+        pair = lax.div(where_to, 2)
+        pltpu.make_async_copy(
+            blocks[mask], w_all.at[pair, :, pl.ds(at, wide // 2)], sems.at[pair]
+        ).start()
     rows = own.shape[0]
     half = rows // 2
     for slot, shift in enumerate((2, 1, 3, 0)):
         start = pl.multiple_of(slot_row(ids, shift, rows), rows)
         x_all[slot * rows : (slot + 1) * rows, :] = context[pl.ds(start, rows), :]
-    wide = w_all.shape[2]
-
-    @pl.loop(0, 8)
+
+    @pl.loop(0, 4)
     def _(n):
-        pltpu.make_async_copy(w_all.at[n], w_all.at[n], sems.at[n]).wait()
+        arrived(w_all.at[n], sems.at[n])
         columns = pl.ds(pl.multiple_of(n * wide, wide), wide)
         part = jnp.dot(x_all[...], w_all[n], preferred_element_type=jnp.float32).astype(own.dtype)
         for k, ref in enumerate(
@@ -389,11 +424,7 @@
     return 0.5 * v * (1.0 + jnp.tanh(0.7978845608028654 * (v + 0.044715 * (v * v * v))))
 
 
-def feed_kernel(order, ids, *refs):
-    pieces = refs[:8]
-    blocks = refs[8:18]
-    outs = refs[18:25]
-    x_all, hidden, gate, up, down, sems = refs[25:]
+def gate_up(order, ids, blocks, rows, hidden, gate, up, sems):
     units, _, wide = gate.shape
     lead = 2
     for low, high, sem in ((0, lead, 0), (lead, units, 1)):
@@ -402,26 +433,54 @@
             order, ids, blocks, 3 * units, units + low, units + high,
             into_rows(up, units), sems.at[sem],
         )
-    fetch(order, ids, blocks, 3 * units, 2 * units, 3 * units, into_blocks(down, 2 * units), sems.at[2])
-    rows = pieces[0].shape[0]
-    for k, piece in enumerate((6, 7, 4, 5, 2, 3, 0, 1)):
-        x_all[k * rows : (k + 1) * rows, :] = pieces[piece][...]
+    yield
     for j in range(units):
         if j in (0, lead):
             part = pl.ds(j, lead if j == 0 else units - lead)
             arrived(gate.at[part], sems.at[j // lead])
             arrived(up.at[part], sems.at[j // lead])
-        gated = jnp.dot(x_all[...], gate[j], preferred_element_type=jnp.float32)
-        upped = jnp.dot(x_all[...], up[j], preferred_element_type=jnp.float32)
+        gated = jnp.dot(rows[...], gate[j], preferred_element_type=jnp.float32)
+        upped = jnp.dot(rows[...], up[j], preferred_element_type=jnp.float32)
         hidden[:, j * wide : (j + 1) * wide] = (gelu(gated) * upped).astype(hidden.dtype)
+
+
+def near_kernel(order, ids, *refs):
+    pieces, blocks = refs[:6], refs[6:16]
+    hidden, x_all, gate, up, sems = refs[16:]
+    work = gate_up(order, ids, blocks, x_all, hidden, gate, up, sems)
+    next(work)
+    rows = pieces[0].shape[0]
+    for k, piece in enumerate((4, 5, 2, 3, 0, 1)):
+        x_all[k * rows : (k + 1) * rows, :] = pieces[piece][...]
+    for _ in work:
+        pass
+
+
+def feed_kernel(order, ids, near, *refs):
+    pieces, blocks = refs[:2], refs[2:12]
+    outs = refs[12:19]
+    x_all, hidden, gate, up, down, sems = refs[19:]
+    units, _, wide = gate.shape
+    rows = pieces[0].shape[0]
+    work = gate_up(order, ids, blocks, x_all, hidden, gate, up, sems)
+    next(work)
+    fetch(order, ids, blocks, 3 * units, 2 * units, 3 * units, into_blocks(down, 2 * units), sems.at[2])
+    for k in range(2):
+        x_all[k * rows : (k + 1) * rows, :] = pieces[k][...]
+    for _ in work:
+        pass
     arrived(down, sems.at[2])
     for n in range(8):
-        part = jnp.dot(
-            hidden[...], down[n].reshape(units * wide, wide), preferred_element_type=jnp.float32
-        ).astype(outs[0].dtype)
-        for k in range(6):
-            outs[k][:, n * wide : (n + 1) * wide] = part[k * rows : (k + 1) * rows, :]
-        outs[6][:, n * wide : (n + 1) * wide] = part[6 * rows :, :]
+        columns = slice(n * wide, (n + 1) * wide)
+        weights = down[n].reshape(units * wide, wide)
+        far = jnp.dot(hidden[...], weights, preferred_element_type=jnp.float32)
+        rest = jnp.dot(near[...], weights, preferred_element_type=jnp.float32)
+        far, rest = far.astype(outs[0].dtype), rest.astype(outs[0].dtype)
+        for k in range(2):
+            outs[k][:, columns] = far[k * rows : (k + 1) * rows, :]
+        for k in range(4):
+            outs[2 + k][:, columns] = rest[k * rows : (k + 1) * rows, :]
+        outs[6][:, columns] = rest[4 * rows :, :]
 
 
 def residual(base, shares, half):
@@ -469,9 +528,15 @@
     return pl.BlockSpec(array.shape, lambda *_: (0,) * len(array.shape))
 
 
+def room(array):
+    sized = hasattr(array, "dtype") and array.dtype in (jnp.bfloat16, jnp.float32)
+    return math.prod(array.shape) * jnp.dtype(array.dtype).itemsize if sized else 0
+
+
 def call(kernel, scalars, arrays, raw, outs, scratch, flops, moved):
     single = not isinstance(outs, (list, tuple))
     out_list = [outs] if single else list(outs)
+    held = 2 * sum(map(room, [*arrays, *out_list])) + sum(map(room, scratch))
     result = pl.pallas_call(
       kernel,
       out_shape=out_list,
@@ -484,6 +549,7 @@
           scratch_shapes=scratch,
       ),
       cost_estimate=pl.CostEstimate(flops=flops, bytes_accessed=moved, transcendentals=0),
+      compiler_params=pltpu.CompilerParams(vmem_limit_bytes=held + SPARE),
     )(*scalars, *arrays, *raw)
     return result[0] if single else result
 
@@ -573,25 +639,26 @@
     row_f32 = shape((rows, width), f32)
 
     qkv_own = call(
-        pack_kernel, [], [w_query, w_key, w_value], [],
-        shape((3 * inner // block, block, block), bf16), [], 2 * block * inner, 12 * block * inner,
+        pack_kernel, [], [], [w_query, w_key, w_value],
+        shape((3 * inner // block, block, block), bf16), [pltpu.SemaphoreType.DMA((1,))], 2 * block * inner, 12 * block * inner,
     )
     low, high = call(
-        rms_kernel, [], [hidden_states, gain_attn.reshape(1, width)], [],
-        [half_bf, half_bf], [], 4 * rows * width, 6 * rows * width,
+        rms_kernel, [], [gain_attn.reshape(1, width)], [hidden_states],
+        [half_bf, half_bf],
+        [pltpu.VMEM((rows, width), f32), pltpu.SemaphoreType.DMA((2,))], 4 * rows * width, 6 * rows * width,
     )
     normed = half_gather(low, high)
     qkv = plane_gather_split(qkv_own)
     out_blocks = plane_gather(w_out)
     feed_own = call(
-        pack_kernel, [], [w_gate, w_up, w_down], [],
-        shape((3 * hidden // block, block, block), bf16), [], 2 * block * hidden, 12 * block * hidden,
+        pack_kernel, [], [], [w_gate, w_up, w_down],
+        shape((3 * hidden // block, block, block), bf16), [pltpu.SemaphoreType.DMA((1,))], 2 * block * hidden, 12 * block * hidden,
     )
     feed = plane_gather_split(feed_own)
 
-    projected = call(
+    queries, keys, values = call(
         project_kernel, [shard_order, ids], normed, qkv,
-        shape((length_all, 3 * inner), bf16),
+        [shape((length_all, inner), bf16)] * 3,
         [
             pltpu.VMEM((length_all, width), bf16),
             pltpu.VMEM((3 * inner // block, width, block), bf16),
@@ -600,22 +667,23 @@
         6 * length_all * width * inner, 6 * width * inner,
     )
 
-    heads = rel_bias.shape[1]
     relative = jnp.arange(4 * TILE, dtype=jnp.int32) - 2 * TILE
     onehot = (
         bucket_index(relative)[:, None]
         == jnp.arange(rel_bias.shape[0], dtype=jnp.int32)[None, :]
     ).astype(f32)
     bias_table = jnp.dot(onehot, rel_bias, precision=lax.Precision.HIGHEST).T
-    context = attention(lengths, projected, bias_table.reshape(heads // 2, 2, 4 * TILE))
+    context = attention(
+        lengths, queries, keys, values, bias_table
+    )
 
     parts = call(
         out_kernel, [shard_order, ids], [context], out_blocks,
         [half_bf] * 6 + [row_bf],
         [
             pltpu.VMEM((length_all, inner), bf16),
-            pltpu.VMEM((8, inner, block), bf16),
-            pltpu.SemaphoreType.DMA((8,)),
+            pltpu.VMEM((4, inner, 2 * block), bf16),
+            pltpu.SemaphoreType.DMA((4,)),
         ],
         2 * length_all * width * inner, 2 * width * inner,
     )
@@ -627,17 +695,25 @@
     normed = half_gather(low, high)
 
     units = hidden // block
+    weights = pltpu.VMEM((units, width, block), bf16)
+    near = call(
+        near_kernel, [shard_order, ids], normed[:6], feed,
+        shape((3 * rows, hidden), bf16),
+        [pltpu.VMEM((3 * rows, width), bf16), weights, weights, pltpu.SemaphoreType.DMA((2,))],
+        12 * rows * width * hidden, 4 * width * hidden,
+    )
     parts = call(
-        feed_kernel, [shard_order, ids], normed, feed, [half_bf] * 6 + [row_bf],
+        feed_kernel, [shard_order, ids], [near, *normed[6:]], feed,
+        [half_bf] * 6 + [row_bf],
         [
-            pltpu.VMEM((length_all, width), bf16),
-            pltpu.VMEM((length_all, hidden), bf16),
-            pltpu.VMEM((units, width, block), bf16),
-            pltpu.VMEM((units, width, block), bf16),
+            pltpu.VMEM((rows, width), bf16),
+            pltpu.VMEM((rows, hidden), bf16),
+            weights,
+            weights,
             pltpu.VMEM((8, units, block, block), bf16),
             pltpu.SemaphoreType.DMA((3,)),
         ],
-        6 * length_all * width * hidden, 6 * width * hidden,
+        12 * rows * width * hidden, 6 * width * hidden,
     )
     shares = half_scatter(*parts)
     output_rows, pool = call(
@@ -646,8 +722,8 @@
         [row_f32, shape((8, TILE), f32)], [], 8 * rows * width, 16 * rows * width,
     )
     total = pool
-    for step in (1, 2):
-        total = total + lax.ppermute(total, "tensor", [(i, i ^ step) for i in range(4)])
+    for step in (1, 2, 3):
+        total = total + lax.ppermute(pool, "tensor", [(i, i ^ step) for i in range(4)])
     reward = total / lengths[0].astype(f32)
     moments = jnp.where(lax.broadcasted_iota(jnp.int32, reward.shape, 0) == 0, reward, reward * reward)
     for mask in (1, 2, 4):

time: 272 us -> 261 us (0.960)
  Pallas kernels: 54.5 us -> 32.5 us
  local copies, waits for them, and re-layouts: 9.86 us -> 20.8 us
  starting transfers between devices: 49.6 us -> 55.8 us
  other arithmetic: 5.47 us -> 0.43 us
    ppermute x28, waiting for transfers between devices: 22.1 us -> 42.2 us  [exchange(): return lax.ppermute(block, 'dp', [(i, i ^ mask) for i in range(8)])]
    ppermute x24, waiting for transfers between devices: 118 us -> 97.7 us  [shift_rows(): return lax.ppermute(block, 'tensor', ring_pairs(step))]
    pallas_call x8 -> x9, Pallas kernels: 43.4 us -> 27.3 us  [call(): pl.pallas_call(kernel, out_shape=out_list, grid_spec=pltpu.PrefetchScalar...]
    unnamed x62 -> x84, local copies, waits for them, and re-layouts: 4.56 us -> 17.3 us
    pallas_call x1, Pallas kernels: 11.1 us -> 5.2 us  [attention(): pl.pallas_call(attention_kernel, out_shape=jax.ShapeDtypeStruct((span, in...]
    ppermute x24, starting transfers between devices: 28.2 us -> 33.9 us  [shift_rows(): return lax.ppermute(block, 'tensor', ring_pairs(step))]
    convert_element_type x4, other arithmetic: 4.09 us -> 0.26 us  [add_share(): (mine.astype(jnp.float32) + received.astype(jnp.float32)).astype(mine.dtype)]
    ppermute x2 -> x3, waiting for transfers between devices: 5.81 us -> 3.94 us  [layer(): lax.ppermute(pool, 'tensor', [(i, i ^ step) for i in range(4)])]
  transfers between devices with their start and end apart: 54 -> 55, of which waited for: 30 -> 28; matrix products, arithmetic and copies ran while one was open for 4% -> 2% of each run, Pallas kernels for 13% -> 8%
where the time goes in v2:
time: 261 us
  waiting for transfers between devices  144 us (55%)
  starting transfers between devices  55.8 us (21%)
  Pallas kernels  32.5 us (12%)
  local copies, waits for them, and re-layouts  20.8 us (8%)
  between operations  6.35 us (2%)
    ppermute x24, waiting for transfers between devices, shift_rows(): return lax.ppermute(block, 'tensor', ring_pairs(step))  97.7 us
    ppermute x28, waiting for transfers between devices, exchange(): return lax.ppermute(block, 'dp', [(i, i ^ mask) for i in range(8)])  42.2 us
    ppermute x24, starting transfers between devices, shift_rows(): return lax.ppermute(block, 'tensor', ring_pairs(step))  33.9 us
    pallas_call x9, Pallas kernels, call(): pl.pallas_call(kernel, out_shape=out_list, grid_spec=pltpu.PrefetchScalar...  27.3 us
    unnamed x84, local copies, waits for them, and re-layouts  17.3 us
    ppermute x28, starting transfers between devices, exchange(): return lax.ppermute(block, 'dp', [(i, i ^ mask) for i in range(8)])  17.1 us
  transfers between devices with their start and end apart: 55, of which 28 were waited for; matrix products, arithmetic and copies ran while one was open for 2% of the time, Pallas kernels for 8%

profile of v2, /device:TPU:0, one launch (start us, length us, event | category | flops | bytes accessed | tf_op | source)
XLA Modules:
  0.0 260.8 jit_solution(9293107321298259202)
XLA Ops:
  16.5 6.7 %collective-permute-done.1.refs_3_ = bf16[64,2048]{1,0:T(8,128)(2,1)S(1)} collective-permute-done((bf16[64,2048]{1,0:T(8,128)(2,1)S(1)}, bf16[64,2048]{1,0:T(8,128)(2,1)S(1)}, u32[]{:S(2)}, u32[]{:S(2)}) %collective-permute-start.1) | collective-permute-done | bytes 262176 | tf_op jit(solution)/shard_map/ppermute | solution.py:558
  28.1 3.8 %collective-permute-done.3.refs_5_ = bf16[64,2048]{1,0:T(8,128)(2,1)S(1)} collective-permute-done((bf16[64,2048]{1,0:T(8,128)(2,1)S(1)}, bf16[64,2048]{1,0:T(8,128)(2,1)S(1)}, u32[]{:S(2)}, u32[]{:S(2)}) %collective-permute-start.3) | collective-permute-done | bytes 262176 | tf_op jit(solution)/shard_map/ppermute | solution.py:558
  37.4 8.0 %collective-permute-done.18.refs_4_ = bf16[512,256]{1,0:T(8,128)(2,1)S(1)} collective-permute-done((bf16[512,256]{1,0:T(8,128)(2,1)}, bf16[512,256]{1,0:T(8,128)(2,1)S(1)}, u32[]{:S(2)}, u32[]{:S(2)}) %collective-permute-start.18) | collective-permute-done | bytes 262176 | tf_op jit(solution)/shard_map/ppermute | solution.py:562
  59.8 3.7 %collective-permute-done.11.refs_14_ = bf16[3,256,256]{2,1,0:T(8,128)(2,1)} collective-permute-done((bf16[3,256,256]{2,1,0:T(8,128)(2,1)S(1)}, bf16[3,256,256]{2,1,0:T(8,128)(2,1)}, u32[]{:S(2)}, u32[]{:S(2)}) %collective-permute-start.11) | collective-permute-done | bytes 393248 | tf_op jit(solution)/shard_map/ppermute | solution.py:562
  80.3 5.7 %shard_map.160 = (bf16[512,512]{1,0:T(8,128)(2,1)S(1)}, bf16[512,512]{1,0:T(8,128)(2,1)S(1)}, bf16[512,512]{1,0:T(8,128)(2,1)S(1)}) custom-call(s32[8]{0:T(128)S(1)} %copy-done.13, s32[2]{0:T(128)S(1)} %pad_add_fusion.ids, bf16[64,2048]{1,0:T(8,128)(2,1)S(1)} %copy-done.20, bf16[64,2048]{1,0:T(8,128)(2,1)S(1)} %copy-done.22, ...), custom_call_target="tpu_custom_call" | custom-call | flops 3221225472 | bytes 6291456 | tf_op jit(solution)/shard_map/pallas_call | solution.py:540
  86.0 5.2 %attention.1.context = bf16[512,512]{1,0:T(8,128)(2,1)S(1)} custom-call(s32[1]{0:T(128)S(6)} %copy.17.length_ref.length, bf16[512,512]{1,0:T(8,128)(2,1)S(1)} %get-tuple-element.28.q_ref, bf16[512,512]{1,0:T(8,128)(2,1)S(1)} %get-tuple-element.29.k_ref, bf16[512,512]{1,0:T(8,128)(2,1)S(1)} %get-tuple-element.30.v_ref, f32[8,512]{1,0:T(8,128)S(1)} %copy-done.41), custom_call_target="tpu_custom_call" | custom-call | flops 2147483648 | bytes 2097152 | tf_op jit(solution)/shard_map/attention/pallas_call | solution.py:175
  94.5 10.5 %collective-permute-done.22 = bf16[64,2048]{1,0:T(8,128)(2,1)S(1)} collective-permute-done((bf16[64,2048]{1,0:T(8,128)(2,1)S(1)}, bf16[64,2048]{1,0:T(8,128)(2,1)S(1)}, u32[]{:S(2)}, u32[]{:S(2)}) %collective-permute-start.22) | collective-permute-done | bytes 262176 | tf_op jit(solution)/shard_map/ppermute | solution.py:558
  105.1 5.6 %collective-permute-done.24.refs_2_ = bf16[64,2048]{1,0:T(8,128)(2,1)S(1)} collective-permute-done((bf16[64,2048]{1,0:T(8,128)(2,1)S(1)}, bf16[64,2048]{1,0:T(8,128)(2,1)S(1)}, u32[]{:S(2)}, u32[]{:S(2)}) %collective-permute-start.24) | collective-permute-done | bytes 262176 | tf_op jit(solution)/shard_map/ppermute | solution.py:558
  110.7 5.2 %collective-permute-done.26 = bf16[64,2048]{1,0:T(8,128)(2,1)S(1)} collective-permute-done((bf16[64,2048]{1,0:T(8,128)(2,1)S(1)}, bf16[64,2048]{1,0:T(8,128)(2,1)S(1)}, u32[]{:S(2)}, u32[]{:S(2)}) %collective-permute-start.26) | collective-permute-done | bytes 262176 | tf_op jit(solution)/shard_map/ppermute | solution.py:558
  116.4 3.4 %collective-permute-start.27 = (bf16[64,2048]{1,0:T(8,128)(2,1)S(1)}, bf16[64,2048]{1,0:T(8,128)(2,1)S(1)}, u32[]{:S(2)}, u32[]{:S(2)}) collective-permute-start(bf16[64,2048]{1,0:T(8,128)(2,1)S(1)} %add_convert_fusion.2), channel_id=1, source_target_pairs={{0,3},{1,0},{2,1},{3,2},{4,7},{5,4},{6,5},{7,6},{8,11},{9,8},{10,9... | collective-permute-start | bytes 786440 | tf_op jit(solution)/shard_map/ppermute | solution.py:558
  121.1 5.5 %collective-permute-done.25.refs_3_ = bf16[64,2048]{1,0:T(8,128)(2,1)S(1)} collective-permute-done((bf16[64,2048]{1,0:T(8,128)(2,1)S(1)}, bf16[64,2048]{1,0:T(8,128)(2,1)S(1)}, u32[]{:S(2)}, u32[]{:S(2)}) %collective-permute-start.25) | collective-permute-done | bytes 262176 | tf_op jit(solution)/shard_map/ppermute | solution.py:558
  128.2 4.4 %collective-permute-done.27.refs_4_ = bf16[64,2048]{1,0:T(8,128)(2,1)S(1)} collective-permute-done((bf16[64,2048]{1,0:T(8,128)(2,1)S(1)}, bf16[64,2048]{1,0:T(8,128)(2,1)S(1)}, u32[]{:S(2)}, u32[]{:S(2)}) %collective-permute-start.27) | collective-permute-done | bytes 262176 | tf_op jit(solution)/shard_map/ppermute | solution.py:558
  134.1 12.9 %collective-permute-done.37.refs_12_.refs_8_ = bf16[8,256,256]{2,1,0:T(8,128)(2,1)S(1)} collective-permute-done((bf16[8,256,256]{2,1,0:T(8,128)(2,1)S(1)}, bf16[8,256,256]{2,1,0:T(8,128)(2,1)S(1)}, u32[]{:S(2)}, u32[]{:S(2)}) %collective-permute-start.37) | collective-permute-done | bytes 1048608 | tf_op jit(solution)/shard_map/ppermute | solution.py:562
  146.9 8.0 %collective-permute-done.38.refs_13_.refs_9_ = bf16[7,256,256]{2,1,0:T(8,128)(2,1)S(1)} collective-permute-done((bf16[7,256,256]{2,1,0:T(8,128)(2,1)S(1)}, bf16[7,256,256]{2,1,0:T(8,128)(2,1)S(1)}, u32[]{:S(2)}, u32[]{:S(2)}) %collective-permute-start.38) | collective-permute-done | bytes 917536 | tf_op jit(solution)/shard_map/ppermute | solution.py:562
  155.4 10.0 %collective-permute-done.29.refs_3_ = bf16[64,2048]{1,0:T(8,128)(2,1)S(1)} collective-permute-done((bf16[64,2048]{1,0:T(8,128)(2,1)S(1)}, bf16[64,2048]{1,0:T(8,128)(2,1)S(1)}, u32[]{:S(2)}, u32[]{:S(2)}) %collective-permute-start.29) | collective-permute-done | bytes 262176 | tf_op jit(solution)/shard_map/ppermute | solution.py:558
  165.4 7.9 %collective-permute-done.30.refs_4_ = bf16[64,2048]{1,0:T(8,128)(2,1)S(1)} collective-permute-done((bf16[64,2048]{1,0:T(8,128)(2,1)S(1)}, bf16[64,2048]{1,0:T(8,128)(2,1)S(1)}, u32[]{:S(2)}, u32[]{:S(2)}) %collective-permute-start.30) | collective-permute-done | bytes 262176 | tf_op jit(solution)/shard_map/ppermute | solution.py:558
  175.4 6.2 %collective-permute-done.31.refs_5_ = bf16[64,2048]{1,0:T(8,128)(2,1)S(1)} collective-permute-done((bf16[64,2048]{1,0:T(8,128)(2,1)S(1)}, bf16[64,2048]{1,0:T(8,128)(2,1)S(1)}, u32[]{:S(2)}, u32[]{:S(2)}) %collective-permute-start.31) | collective-permute-done | bytes 262176 | tf_op jit(solution)/shard_map/ppermute | solution.py:558
  181.5 4.3 %collective-permute-start.42 = (bf16[64,2048]{1,0:T(8,128)(2,1)S(1)}, bf16[64,2048]{1,0:T(8,128)(2,1)S(1)}, u32[]{:S(2)}, u32[]{:S(2)}) collective-permute-start(bf16[64,2048]{1,0:T(8,128)(2,1)S(1)} %collective-permute-done.31.refs_5_), channel_id=1, source_target_pairs={{0,3},{1,0},{2,1},{3,2},{4,7},{5,4},{6,5},{7,6},{8,11},{9,8},{10,9... | collective-permute-start | bytes 786440 | tf_op jit(solution)/shard_map/ppermute | solution.py:558
  185.8 6.7 %shard_map.164.near = bf16[384,1280]{1,0:T(8,128)(2,1)S(1)} custom-call(s32[8]{0:T(128)S(1)} %copy-done.13, s32[2]{0:T(128)S(1)} %pad_add_fusion.ids, bf16[64,2048]{1,0:T(8,128)(2,1)S(1)} %get-tuple-element.39.refs_0_, bf16[64,2048]{1,0:T(8,128)(2,1)S(1)} %get-tuple-element.40.refs_1_, bf16[64,2048]{1,0:T(8,128)(2,1)S(1)} %collective-permute-done.28.refs_2_, ...), custom_call_target="tpu_custom_call" | custom-call | flops 4026531840 | bytes 10485760 | tf_op jit(solution)/shard_map/pallas_call | solution.py:540
  192.6 8.4 %shard_map.165 = (bf16[64,2048]{1,0:T(8,128)(2,1)S(1)}, bf16[64,2048]{1,0:T(8,128)(2,1)S(1)}, bf16[64,2048]{1,0:T(8,128)(2,1)S(1)}, bf16[64,2048]{1,0:T(8,128)(2...) custom-call(s32[8]{0:T(128)S(1)} %copy-done.13, ...), custom_call_target="tpu_custom_call" | custom-call | flops 4026531840 | bytes 15728640 | tf_op jit(solution)/shard_map/pallas_call | solution.py:540
  207.6 5.0 %collective-permute-done.43 = bf16[64,2048]{1,0:T(8,128)(2,1)S(1)} collective-permute-done((bf16[64,2048]{1,0:T(8,128)(2,1)S(1)}, bf16[64,2048]{1,0:T(8,128)(2,1)S(1)}, u32[]{:S(2)}, u32[]{:S(2)}) %collective-permute-start.43) | collective-permute-done | bytes 262176 | tf_op jit(solution)/shard_map/ppermute | solution.py:558
  213.1 14.3 %collective-permute-done.47 = bf16[64,2048]{1,0:T(8,128)(2,1)S(1)} collective-permute-done((bf16[64,2048]{1,0:T(8,128)(2,1)S(1)}, bf16[64,2048]{1,0:T(8,128)(2,1)S(1)}, u32[]{:S(2)}, u32[]{:S(2)}) %collective-permute-start.47) | collective-permute-done | bytes 262176 | tf_op jit(solution)/shard_map/ppermute | solution.py:558
  227.5 4.3 %collective-permute-start.48 = (bf16[64,2048]{1,0:T(8,128)(2,1)S(1)}, bf16[64,2048]{1,0:T(8,128)(2,1)S(1)}, u32[]{:S(2)}, u32[]{:S(2)}) collective-permute-start(bf16[64,2048]{1,0:T(8,128)(2,1)S(1)} %add_convert_fusion), channel_id=1, source_target_pairs={{0,3},{1,0},{2,1},{3,2},{4,7},{5,4},{6,5},{7,6},{8,11},{9,8},{10,9... | collective-permute-start | bytes 786440 | tf_op jit(solution)/shard_map/ppermute | solution.py:558
  238.4 4.3 %collective-permute-start.51 = (f32[8,128]{1,0:T(8,128)S(1)}, f32[8,128]{1,0:T(8,128)S(1)}, u32[]{:S(2)}, u32[]{:S(2)}) collective-permute-start(f32[8,128]{1,0:T(8,128)S(1)} %get-tuple-element.49), channel_id=1, source_target_pairs={{0,3},{1,2},{2,1},{3,0},{4,7},{5,6},{6,5},{7,4},{8,11},{9,10},{10,... | collective-permute-start | bytes 12296 | tf_op jit(solution)/shard_map/ppermute | solution.py:726
  (198 shorter events, 94.6 us)
Async XLA Ops:
  9.0 38.7 %collective-permute-start.7 = (bf16[6,256,256]{2,1,0:T(8,128)(2,1)S(1)}, bf16[6,256,256]{2,1,0:T(8,128)(2,1)S(1)}, u32[]{:S(2)}, u32[]{:S(2)}) collective-permute-start(bf16[6,256,256]{2,1,0:T(8,128)(2,1)S(1)} %shard_map.159.refs_8_), channel_id=1, source_target_pairs={{0,8},{4,12},{8,0},{12,4},{16,24},{20,28},{24,16},{28,20},{1,9},{5... | collective-permute-start | bytes 2359304 | tf_op jit(solution)/shard_map/ppermute | solution.py:562
  10.6 40.1 %collective-permute-start.9 = (bf16[6,256,256]{2,1,0:T(8,128)(2,1)S(1)}, bf16[6,256,256]{2,1,0:T(8,128)(2,1)}, u32[]{:S(2)}, u32[]{:S(2)}) collective-permute-start(bf16[6,256,256]{2,1,0:T(8,128)(2,1)S(1)} %shard_map.159.refs_8_), channel_id=1, source_target_pairs={{0,16},{4,20},{8,24},{12,28},{16,0},{20,4},{24,8},{28,12},{1,17},{... | collective-permute-start | bytes 2359304 | tf_op jit(solution)/shard_map/ppermute | solution.py:562
  32.8 32.8 %collective-permute-start.6 = (bf16[6,256,256]{2,1,0:T(8,128)(2,1)S(1)}, bf16[6,256,256]{2,1,0:T(8,128)(2,1)S(1)}, u32[]{:S(2)}, u32[]{:S(2)}) collective-permute-start(bf16[6,256,256]{2,1,0:T(8,128)(2,1)S(1)} %shard_map.159.refs_8_), channel_id=1, source_target_pairs={{0,4},{4,0},{8,12},{12,8},{16,20},{20,16},{24,28},{28,24},{1,5},{5... | collective-permute-start | bytes 2359304 | tf_op jit(solution)/shard_map/ppermute | solution.py:562
  35.0 16.8 %collective-permute-start.20 = (bf16[512,256]{1,0:T(8,128)(2,1)}, bf16[512,256]{1,0:T(8,128)(2,1)S(1)}, u32[]{:S(2)}, u32[]{:S(2)}) collective-permute-start(bf16[512,256]{1,0:T(8,128)(2,1)} %refs_0_.4), channel_id=1, source_target_pairs={{0,24},{4,28},{8,16},{12,20},{16,8},{20,12},{24,0},{28,4},{1,25},{... | collective-permute-start | bytes 786440 | tf_op jit(solution)/shard_map/ppermute | solution.py:562
  50.7 18.4 %collective-permute-start.8 = (bf16[6,256,256]{2,1,0:T(8,128)(2,1)S(1)}, bf16[6,256,256]{2,1,0:T(8,128)(2,1)}, u32[]{:S(2)}, u32[]{:S(2)}) collective-permute-start(bf16[6,256,256]{2,1,0:T(8,128)(2,1)S(1)} %collective-permute-done.7.refs_10_), channel_id=1, source_target_pairs={{0,4},{4,0},{8,12},{12,8},{16,20},{20,16},{24,28},{28,24},{1,5},{5... | collective-permute-start | bytes 2359304 | tf_op jit(solution)/shard_map/ppermute | solution.py:562
  66.5 49.9 %collective-permute-start.35 = (bf16[15,256,256]{2,1,0:T(8,128)(2,1)S(1)}, bf16[15,256,256]{2,1,0:T(8,128)(2,1)}, u32[]{:S(2)}, u32[]{:S(2)}) collective-permute-start(bf16[15,256,256]{2,1,0:T(8,128)(2,1)S(1)} %shard_map.163.refs_6_.refs_2_), channel_id=1, source_target_pairs={{0,16},{4,20},{8,24},{12,28},{16,0},{20,4},{24,8},{28,12},{1,17},{... | collective-permute-start | bytes 5898248 | tf_op jit(solution)/shard_map/ppermute | solution.py:562
  69.1 58.5 %collective-permute-start.33 = (bf16[15,256,256]{2,1,0:T(8,128)(2,1)S(1)}, bf16[15,256,256]{2,1,0:T(8,128)(2,1)S(1)}, u32[]{:S(2)}, u32[]{:S(2)}) collective-permute-start(bf16[15,256,256]{2,1,0:T(8,128)(2,1)S(1)} %shard_map.163.refs_6_.refs_2_), channel_id=1, source_target_pairs={{0,8},{4,12},{8,0},{12,4},{16,24},{20,28},{24,16},{28,20},{1,9},{5... | collective-permute-start | bytes 5898248 | tf_op jit(solution)/shard_map/ppermute | solution.py:562
  70.9 20.4 %collective-permute-start.17 = (bf16[512,256]{1,0:T(8,128)(2,1)}, bf16[512,256]{1,0:T(8,128)(2,1)S(1)}, u32[]{:S(2)}, u32[]{:S(2)}) collective-permute-start(bf16[512,256]{1,0:T(8,128)(2,1)} %copy-done.23), channel_id=1, source_target_pairs={{0,4},{4,0},{8,12},{12,8},{16,20},{20,16},{24,28},{28,24},{1,5},{5... | collective-permute-start | bytes 786440 | tf_op jit(solution)/shard_map/ppermute | solution.py:562
  70.9 20.3 %collective-permute-start.19 = (bf16[512,256]{1,0:T(8,128)(2,1)}, bf16[512,256]{1,0:T(8,128)(2,1)S(1)}, u32[]{:S(2)}, u32[]{:S(2)}) collective-permute-start(bf16[512,256]{1,0:T(8,128)(2,1)} %copy-done.27), channel_id=1, source_target_pairs={{0,4},{4,0},{8,12},{12,8},{16,20},{20,16},{24,28},{28,24},{1,5},{5... | collective-permute-start | bytes 786440 | tf_op jit(solution)/shard_map/ppermute | solution.py:562
  71.4 19.8 %collective-permute-start.21 = (bf16[512,256]{1,0:T(8,128)(2,1)}, bf16[512,256]{1,0:T(8,128)(2,1)S(1)}, u32[]{:S(2)}, u32[]{:S(2)}) collective-permute-start(bf16[512,256]{1,0:T(8,128)(2,1)} %copy-done.33), channel_id=1, source_target_pairs={{0,4},{4,0},{8,12},{12,8},{16,20},{20,16},{24,28},{28,24},{1,5},{5... | collective-permute-start | bytes 786440 | tf_op jit(solution)/shard_map/ppermute | solution.py:562
  94.0 39.5 %collective-permute-start.32 = (bf16[15,256,256]{2,1,0:T(8,128)(2,1)S(1)}, bf16[15,256,256]{2,1,0:T(8,128)(2,1)S(1)}, u32[]{:S(2)}, u32[]{:S(2)}) collective-permute-start(bf16[15,256,256]{2,1,0:T(8,128)(2,1)S(1)} %shard_map.163.refs_6_.refs_2_), channel_id=1, source_target_pairs={{0,4},{4,0},{8,12},{12,8},{16,20},{20,16},{24,28},{28,24},{1,5},{5... | collective-permute-start | bytes 5898248 | tf_op jit(solution)/shard_map/ppermute | solution.py:562
  94.5 16.2 %collective-permute-start.24 = (bf16[64,2048]{1,0:T(8,128)(2,1)S(1)}, bf16[64,2048]{1,0:T(8,128)(2,1)S(1)}, u32[]{:S(2)}, u32[]{:S(2)}) collective-permute-start(bf16[64,2048]{1,0:T(8,128)(2,1)S(1)} %get-tuple-element.34), channel_id=1, source_target_pairs={{0,1},{1,2},{2,3},{3,0},{4,5},{5,6},{6,7},{7,4},{8,9},{9,10},{10,1... | collective-permute-start | bytes 786440 | tf_op jit(solution)/shard_map/ppermute | solution.py:558
  116.4 16.2 %collective-permute-start.27 = (bf16[64,2048]{1,0:T(8,128)(2,1)S(1)}, bf16[64,2048]{1,0:T(8,128)(2,1)S(1)}, u32[]{:S(2)}, u32[]{:S(2)}) collective-permute-start(bf16[64,2048]{1,0:T(8,128)(2,1)S(1)} %add_convert_fusion.2), channel_id=1, source_target_pairs={{0,3},{1,0},{2,1},{3,2},{4,7},{5,4},{6,5},{7,6},{8,11},{9,8},{10,9... | collective-permute-start | bytes 786440 | tf_op jit(solution)/shard_map/ppermute | solution.py:558
  126.6 20.3 %collective-permute-start.37 = (bf16[8,256,256]{2,1,0:T(8,128)(2,1)S(1)}, bf16[8,256,256]{2,1,0:T(8,128)(2,1)S(1)}, u32[]{:S(2)}, u32[]{:S(2)}) collective-permute-start(bf16[8,256,256]{2,1,0:T(8,128)(2,1)S(1)} %slice.30), channel_id=1, source_target_pairs={{0,8},{4,12},{8,0},{12,4},{16,24},{20,28},{24,16},{28,20},{1,9},{5... | collective-permute-start | bytes 3145736 | tf_op jit(solution)/shard_map/ppermute | solution.py:562
  127.6 58.2 %collective-permute-start.34 = (bf16[15,256,256]{2,1,0:T(8,128)(2,1)S(1)}, bf16[15,256,256]{2,1,0:T(8,128)(2,1)S(1)}, u32[]{:S(2)}, u32[]{:S(2)}) collective-permute-start(bf16[15,256,256]{2,1,0:T(8,128)(2,1)S(1)} %collective-permute-done.33.refs_8_.refs_4_), channel_id=1, source_target_pairs={{0,4},{4,0},{8,12},{12,8},{16,20},{20,16},{24,28},{28,24},{1,5},{5... | collective-permute-start | bytes 5898248 | tf_op jit(solution)/shard_map/ppermute | solution.py:562
  127.6 58.2 %collective-permute-start.36 = (bf16[15,256,256]{2,1,0:T(8,128)(2,1)}, bf16[15,256,256]{2,1,0:T(8,128)(2,1)S(1)}, u32[]{:S(2)}, u32[]{:S(2)}) collective-permute-start(bf16[15,256,256]{2,1,0:T(8,128)(2,1)} %collective-permute-done.35.refs_10_.refs_6_), channel_id=1, source_target_pairs={{0,4},{4,0},{8,12},{12,8},{16,20},{20,16},{24,28},{28,24},{1,5},{5... | collective-permute-start | bytes 5898248 | tf_op jit(solution)/shard_map/ppermute | solution.py:562
  132.6 22.3 %collective-permute-start.38 = (bf16[7,256,256]{2,1,0:T(8,128)(2,1)S(1)}, bf16[7,256,256]{2,1,0:T(8,128)(2,1)S(1)}, u32[]{:S(2)}, u32[]{:S(2)}) collective-permute-start(bf16[7,256,256]{2,1,0:T(8,128)(2,1)S(1)} %slice.31), channel_id=1, source_target_pairs={{0,16},{4,20},{8,24},{12,28},{16,0},{20,4},{24,8},{28,12},{1,17},{... | collective-permute-start | bytes 2752520 | tf_op jit(solution)/shard_map/ppermute | solution.py:562
  133.5 21.3 %collective-permute-start.28 = (bf16[64,2048]{1,0:T(8,128)(2,1)S(1)}, bf16[64,2048]{1,0:T(8,128)(2,1)S(1)}, u32[]{:S(2)}, u32[]{:S(2)}) collective-permute-start(bf16[64,2048]{1,0:T(8,128)(2,1)S(1)} %get-tuple-element.39.refs_0_), channel_id=1, source_target_pairs={{0,1},{1,2},{2,3},{3,0},{4,5},{5,6},{6,7},{7,4},{8,9},{9,10},{10,1... | collective-permute-start | bytes 786440 | tf_op jit(solution)/shard_map/ppermute | solution.py:558
  146.9 38.9 %collective-permute-start.39 = (bf16[8,256,256]{2,1,0:T(8,128)(2,1)S(1)}, bf16[8,256,256]{2,1,0:T(8,128)(2,1)S(1)}, u32[]{:S(2)}, u32[]{:S(2)}) collective-permute-start(bf16[8,256,256]{2,1,0:T(8,128)(2,1)S(1)} %collective-permute-done.37.refs_12_.refs_8_), channel_id=1, source_target_pairs={{0,4},{4,0},{8,12},{12,8},{16,20},{20,16},{24,28},{28,24},{1,5},{5... | collective-permute-start | bytes 3145736 | tf_op jit(solution)/shard_map/ppermute | solution.py:562
  154.9 26.7 %collective-permute-start.40 = (bf16[7,256,256]{2,1,0:T(8,128)(2,1)S(1)}, bf16[7,256,256]{2,1,0:T(8,128)(2,1)S(1)}, u32[]{:S(2)}, u32[]{:S(2)}) collective-permute-start(bf16[7,256,256]{2,1,0:T(8,128)(2,1)S(1)} %collective-permute-done.38.refs_13_.refs_9_), channel_id=1, source_target_pairs={{0,4},{4,0},{8,12},{12,8},{16,20},{20,16},{24,28},{28,24},{1,5},{5... | collective-permute-start | bytes 2752520 | tf_op jit(solution)/shard_map/ppermute | solution.py:562
  203.8 28.0 %collective-permute-start.45 = (bf16[64,2048]{1,0:T(8,128)(2,1)S(1)}, bf16[64,2048]{1,0:T(8,128)(2,1)S(1)}, u32[]{:S(2)}, u32[]{:S(2)}) collective-permute-start(bf16[64,2048]{1,0:T(8,128)(2,1)S(1)} %get-tuple-element.44), channel_id=1, source_target_pairs={{0,1},{1,2},{2,3},{3,0},{4,5},{5,6},{6,7},{7,4},{8,9},{9,10},{10,1... | collective-permute-start | bytes 786440 | tf_op jit(solution)/shard_map/ppermute | solution.py:558
  204.5 27.4 %collective-permute-start.46 = (bf16[64,2048]{1,0:T(8,128)(2,1)S(1)}, bf16[64,2048]{1,0:T(8,128)(2,1)S(1)}, u32[]{:S(2)}, u32[]{:S(2)}) collective-permute-start(bf16[64,2048]{1,0:T(8,128)(2,1)S(1)} %get-tuple-element.45), channel_id=1, source_target_pairs={{0,3},{1,0},{2,1},{3,2},{4,7},{5,4},{6,5},{7,6},{8,11},{9,8},{10,9... | collective-permute-start | bytes 786440 | tf_op jit(solution)/shard_map/ppermute | solution.py:558
  207.6 19.8 %collective-permute-start.47 = (bf16[64,2048]{1,0:T(8,128)(2,1)S(1)}, bf16[64,2048]{1,0:T(8,128)(2,1)S(1)}, u32[]{:S(2)}, u32[]{:S(2)}) collective-permute-start(bf16[64,2048]{1,0:T(8,128)(2,1)S(1)} %get-tuple-element.47), channel_id=1, source_target_pairs={{0,3},{1,0},{2,1},{3,2},{4,7},{5,4},{6,5},{7,6},{8,11},{9,8},{10,9... | collective-permute-start | bytes 786440 | tf_op jit(solution)/shard_map/ppermute | solution.py:558
  212.7 22.2 %collective-permute-start.44 = (bf16[64,2048]{1,0:T(8,128)(2,1)S(1)}, bf16[64,2048]{1,0:T(8,128)(2,1)S(1)}, u32[]{:S(2)}, u32[]{:S(2)}) collective-permute-start(bf16[64,2048]{1,0:T(8,128)(2,1)S(1)} %add_convert_fusion.1), channel_id=1, source_target_pairs={{0,1},{1,2},{2,3},{3,0},{4,5},{5,6},{6,7},{7,4},{8,9},{9,10},{10,1... | collective-permute-start | bytes 786440 | tf_op jit(solution)/shard_map/ppermute | solution.py:558
  (73 other events, 915.4 us)

commit v3 on v2

--- a/solution.py
+++ b/solution.py
@@ -524,6 +524,12 @@
     pool_ref[...] = jnp.broadcast_to(pooled, pool_ref.shape)
 
 
+def standard_kernel(reward, first, second, third, fourth, out):
+    moments = (first[...] + second[...] + third[...] + fourth[...]) / 8
+    mean, square = moments[0:1, 0:1], moments[1:2, 0:1]
+    out[...] = (reward[0:1, 0:1] - mean) / jnp.sqrt(square - mean * mean + 1e-06)
+
+
 def whole(array):
     return pl.BlockSpec(array.shape, lambda *_: (0,) * len(array.shape))
 
@@ -576,8 +582,8 @@
     held = {0: block}
     for mask in (2, 4, 1):
         held[mask] = exchange(block, mask)
+    high = exchange(held[2][cut:], 4)
     low = exchange(held[4][:cut], 2)
-    high = exchange(held[2][cut:], 4)
     for mask in (3, 5):
         held[mask] = exchange(held[mask ^ 1], 1)
     pairs = [exchange(low, 1), exchange(high, 1)]
@@ -726,11 +732,9 @@
         total = total + lax.ppermute(pool, "tensor", [(i, i ^ step) for i in range(4)])
     reward = total / lengths[0].astype(f32)
     moments = jnp.where(lax.broadcasted_iota(jnp.int32, reward.shape, 0) == 0, reward, reward * reward)
-    for mask in (1, 2, 4):
-        moments = moments + exchange(moments, mask)
-    reward_mean = moments[0, 0] / 8
-    reward_var = moments[1, 0] / 8 - reward_mean * reward_mean
-    normalized = (reward[0, 0] - reward_mean) / jnp.sqrt(reward_var + 1e-06)
+    moments = moments + exchange(moments, 1)
+    sums = [moments] + [exchange(moments, mask) for mask in (2, 4, 6)]
+    normalized = call(standard_kernel, [], [reward, *sums], [], shape((1, 1), f32), [], 8192, 20480)
     return (output_rows, jnp.reshape(normalized, (1,)))
 
 

time: 261 us -> 256 us (0.981)
  between operations: 6.35 us -> 1.83 us
  waiting for transfers between devices: 144 us -> 141 us
    ppermute x28 -> x29, waiting for transfers between devices: 42.2 us -> 39.4 us  [exchange(): return lax.ppermute(block, 'dp', [(i, i ^ mask) for i in range(8)])]
    ppermute x28 -> x29, starting transfers between devices: 17.1 us -> 19.2 us  [exchange(): return lax.ppermute(block, 'dp', [(i, i ^ mask) for i in range(8)])]
    pallas_call x9 -> x10, Pallas kernels: 27.3 us -> 27.9 us  [call(): pl.pallas_call(kernel, out_shape=out_list, grid_spec=pltpu.PrefetchScalar...]
  transfers between devices with their start and end apart: 55 -> 56, of which waited for: 28 -> 29; matrix products, arithmetic and copies ran while one was open for 2% -> 1% of each run, Pallas kernels for 8% -> 9%
where the time goes in v3:
time: 256 us; the launch traced here: 255 us
  waiting for transfers between devices  141 us (55%)
  starting transfers between devices  57.9 us (23%)
  Pallas kernels  33.1 us (13%)
  local copies, waits for them, and re-layouts  19.7 us (8%)
    ppermute x24, waiting for transfers between devices, shift_rows(): return lax.ppermute(block, 'tensor', ring_pairs(step))  97.7 us
    ppermute x29, waiting for transfers between devices, exchange(): return lax.ppermute(block, 'dp', [(i, i ^ mask) for i in range(8)])  39.4 us
    ppermute x24, starting transfers between devices, shift_rows(): return lax.ppermute(block, 'tensor', ring_pairs(step))  33.9 us
    pallas_call x10, Pallas kernels, call(): pl.pallas_call(kernel, out_shape=out_list, grid_spec=pltpu.PrefetchScalar...  27.9 us
    ppermute x29, starting transfers between devices, exchange(): return lax.ppermute(block, 'dp', [(i, i ^ mask) for i in range(8)])  19.2 us
    unnamed x84, local copies, waits for them, and re-layouts  17.3 us
    pallas_call x1, Pallas kernels, attention(): pl.pallas_call(attention_kernel, out_shape=jax.ShapeDtypeStruct((span, in...  5.2 us
  transfers between devices with their start and end apart: 56, of which 29 were waited for; matrix products, arithmetic and copies ran while one was open for 1% of the time, Pallas kernels for 9%

profile of v3, /device:TPU:0, one launch (start us, length us, event | category | flops | bytes accessed | tf_op | source)
XLA Modules:
  0.0 254.9 jit_solution(10457505296867936968)
XLA Ops:
  16.5 6.7 %collective-permute-done.1.refs_3_ = bf16[64,2048]{1,0:T(8,128)(2,1)S(1)} collective-permute-done((bf16[64,2048]{1,0:T(8,128)(2,1)S(1)}, bf16[64,2048]{1,0:T(8,128)(2,1)S(1)}, u32[]{:S(2)}, u32[]{:S(2)}) %collective-permute-start.1) | collective-permute-done | bytes 262176 | tf_op jit(solution)/shard_map/ppermute | solution.py:564
  28.1 3.8 %collective-permute-done.3.refs_5_ = bf16[64,2048]{1,0:T(8,128)(2,1)S(1)} collective-permute-done((bf16[64,2048]{1,0:T(8,128)(2,1)S(1)}, bf16[64,2048]{1,0:T(8,128)(2,1)S(1)}, u32[]{:S(2)}, u32[]{:S(2)}) %collective-permute-start.3) | collective-permute-done | bytes 262176 | tf_op jit(solution)/shard_map/ppermute | solution.py:564
  37.4 8.0 %collective-permute-done.18.refs_4_ = bf16[512,256]{1,0:T(8,128)(2,1)S(1)} collective-permute-done((bf16[512,256]{1,0:T(8,128)(2,1)}, bf16[512,256]{1,0:T(8,128)(2,1)S(1)}, u32[]{:S(2)}, u32[]{:S(2)}) %collective-permute-start.18) | collective-permute-done | bytes 262176 | tf_op jit(solution)/shard_map/ppermute | solution.py:568
  59.8 3.7 %collective-permute-done.11.refs_14_ = bf16[3,256,256]{2,1,0:T(8,128)(2,1)} collective-permute-done((bf16[3,256,256]{2,1,0:T(8,128)(2,1)S(1)}, bf16[3,256,256]{2,1,0:T(8,128)(2,1)}, u32[]{:S(2)}, u32[]{:S(2)}) %collective-permute-start.11) | collective-permute-done | bytes 393248 | tf_op jit(solution)/shard_map/ppermute | solution.py:568
  80.3 5.7 %shard_map.160 = (bf16[512,512]{1,0:T(8,128)(2,1)S(1)}, bf16[512,512]{1,0:T(8,128)(2,1)S(1)}, bf16[512,512]{1,0:T(8,128)(2,1)S(1)}) custom-call(s32[8]{0:T(128)S(1)} %copy-done.13, s32[2]{0:T(128)S(1)} %pad_add_fusion.ids, bf16[64,2048]{1,0:T(8,128)(2,1)S(1)} %copy-done.20, bf16[64,2048]{1,0:T(8,128)(2,1)S(1)} %copy-done.22, ...), custom_call_target="tpu_custom_call" | custom-call | flops 3221225472 | bytes 6291456 | tf_op jit(solution)/shard_map/pallas_call | solution.py:546
  86.0 5.2 %attention.1.context = bf16[512,512]{1,0:T(8,128)(2,1)S(1)} custom-call(s32[1]{0:T(128)S(6)} %copy.17.length_ref.length, bf16[512,512]{1,0:T(8,128)(2,1)S(1)} %get-tuple-element.28.q_ref, bf16[512,512]{1,0:T(8,128)(2,1)S(1)} %get-tuple-element.29.k_ref, bf16[512,512]{1,0:T(8,128)(2,1)S(1)} %get-tuple-element.30.v_ref, f32[8,512]{1,0:T(8,128)S(1)} %copy-done.41), custom_call_target="tpu_custom_call" | custom-call | flops 2147483648 | bytes 2097152 | tf_op jit(solution)/shard_map/attention/pallas_call | solution.py:175
  94.5 10.5 %collective-permute-done.22 = bf16[64,2048]{1,0:T(8,128)(2,1)S(1)} collective-permute-done((bf16[64,2048]{1,0:T(8,128)(2,1)S(1)}, bf16[64,2048]{1,0:T(8,128)(2,1)S(1)}, u32[]{:S(2)}, u32[]{:S(2)}) %collective-permute-start.22) | collective-permute-done | bytes 262176 | tf_op jit(solution)/shard_map/ppermute | solution.py:564
  105.0 5.6 %collective-permute-done.24.refs_2_ = bf16[64,2048]{1,0:T(8,128)(2,1)S(1)} collective-permute-done((bf16[64,2048]{1,0:T(8,128)(2,1)S(1)}, bf16[64,2048]{1,0:T(8,128)(2,1)S(1)}, u32[]{:S(2)}, u32[]{:S(2)}) %collective-permute-start.24) | collective-permute-done | bytes 262176 | tf_op jit(solution)/shard_map/ppermute | solution.py:564
  110.7 5.2 %collective-permute-done.26 = bf16[64,2048]{1,0:T(8,128)(2,1)S(1)} collective-permute-done((bf16[64,2048]{1,0:T(8,128)(2,1)S(1)}, bf16[64,2048]{1,0:T(8,128)(2,1)S(1)}, u32[]{:S(2)}, u32[]{:S(2)}) %collective-permute-start.26) | collective-permute-done | bytes 262176 | tf_op jit(solution)/shard_map/ppermute | solution.py:564
  116.4 3.4 %collective-permute-start.27 = (bf16[64,2048]{1,0:T(8,128)(2,1)S(1)}, bf16[64,2048]{1,0:T(8,128)(2,1)S(1)}, u32[]{:S(2)}, u32[]{:S(2)}) collective-permute-start(bf16[64,2048]{1,0:T(8,128)(2,1)S(1)} %add_convert_fusion.2), channel_id=1, source_target_pairs={{0,3},{1,0},{2,1},{3,2},{4,7},{5,4},{6,5},{7,6},{8,11},{9,8},{10,9... | collective-permute-start | bytes 786440 | tf_op jit(solution)/shard_map/ppermute | solution.py:564
  121.1 5.5 %collective-permute-done.25.refs_3_ = bf16[64,2048]{1,0:T(8,128)(2,1)S(1)} collective-permute-done((bf16[64,2048]{1,0:T(8,128)(2,1)S(1)}, bf16[64,2048]{1,0:T(8,128)(2,1)S(1)}, u32[]{:S(2)}, u32[]{:S(2)}) %collective-permute-start.25) | collective-permute-done | bytes 262176 | tf_op jit(solution)/shard_map/ppermute | solution.py:564
  128.2 4.4 %collective-permute-done.27.refs_4_ = bf16[64,2048]{1,0:T(8,128)(2,1)S(1)} collective-permute-done((bf16[64,2048]{1,0:T(8,128)(2,1)S(1)}, bf16[64,2048]{1,0:T(8,128)(2,1)S(1)}, u32[]{:S(2)}, u32[]{:S(2)}) %collective-permute-start.27) | collective-permute-done | bytes 262176 | tf_op jit(solution)/shard_map/ppermute | solution.py:564
  134.0 12.9 %collective-permute-done.37.refs_12_.refs_8_ = bf16[8,256,256]{2,1,0:T(8,128)(2,1)S(1)} collective-permute-done((bf16[8,256,256]{2,1,0:T(8,128)(2,1)S(1)}, bf16[8,256,256]{2,1,0:T(8,128)(2,1)S(1)}, u32[]{:S(2)}, u32[]{:S(2)}) %collective-permute-start.37) | collective-permute-done | bytes 1048608 | tf_op jit(solution)/shard_map/ppermute | solution.py:568
  146.9 8.0 %collective-permute-done.38.refs_13_.refs_9_ = bf16[7,256,256]{2,1,0:T(8,128)(2,1)S(1)} collective-permute-done((bf16[7,256,256]{2,1,0:T(8,128)(2,1)S(1)}, bf16[7,256,256]{2,1,0:T(8,128)(2,1)S(1)}, u32[]{:S(2)}, u32[]{:S(2)}) %collective-permute-start.38) | collective-permute-done | bytes 917536 | tf_op jit(solution)/shard_map/ppermute | solution.py:568
  155.4 10.0 %collective-permute-done.29.refs_3_ = bf16[64,2048]{1,0:T(8,128)(2,1)S(1)} collective-permute-done((bf16[64,2048]{1,0:T(8,128)(2,1)S(1)}, bf16[64,2048]{1,0:T(8,128)(2,1)S(1)}, u32[]{:S(2)}, u32[]{:S(2)}) %collective-permute-start.29) | collective-permute-done | bytes 262176 | tf_op jit(solution)/shard_map/ppermute | solution.py:564
  165.4 7.9 %collective-permute-done.30.refs_4_ = bf16[64,2048]{1,0:T(8,128)(2,1)S(1)} collective-permute-done((bf16[64,2048]{1,0:T(8,128)(2,1)S(1)}, bf16[64,2048]{1,0:T(8,128)(2,1)S(1)}, u32[]{:S(2)}, u32[]{:S(2)}) %collective-permute-start.30) | collective-permute-done | bytes 262176 | tf_op jit(solution)/shard_map/ppermute | solution.py:564
  175.3 6.2 %collective-permute-done.31.refs_5_ = bf16[64,2048]{1,0:T(8,128)(2,1)S(1)} collective-permute-done((bf16[64,2048]{1,0:T(8,128)(2,1)S(1)}, bf16[64,2048]{1,0:T(8,128)(2,1)S(1)}, u32[]{:S(2)}, u32[]{:S(2)}) %collective-permute-start.31) | collective-permute-done | bytes 262176 | tf_op jit(solution)/shard_map/ppermute | solution.py:564
  181.5 4.3 %collective-permute-start.42 = (bf16[64,2048]{1,0:T(8,128)(2,1)S(1)}, bf16[64,2048]{1,0:T(8,128)(2,1)S(1)}, u32[]{:S(2)}, u32[]{:S(2)}) collective-permute-start(bf16[64,2048]{1,0:T(8,128)(2,1)S(1)} %collective-permute-done.31.refs_5_), channel_id=1, source_target_pairs={{0,3},{1,0},{2,1},{3,2},{4,7},{5,4},{6,5},{7,6},{8,11},{9,8},{10,9... | collective-permute-start | bytes 786440 | tf_op jit(solution)/shard_map/ppermute | solution.py:564
  185.8 6.7 %shard_map.164.near = bf16[384,1280]{1,0:T(8,128)(2,1)S(1)} custom-call(s32[8]{0:T(128)S(1)} %copy-done.13, s32[2]{0:T(128)S(1)} %pad_add_fusion.ids, bf16[64,2048]{1,0:T(8,128)(2,1)S(1)} %get-tuple-element.39.refs_0_, bf16[64,2048]{1,0:T(8,128)(2,1)S(1)} %get-tuple-element.40.refs_1_, bf16[64,2048]{1,0:T(8,128)(2,1)S(1)} %collective-permute-done.28.refs_2_, ...), custom_call_target="tpu_custom_call" | custom-call | flops 4026531840 | bytes 10485760 | tf_op jit(solution)/shard_map/pallas_call | solution.py:546
  192.6 8.4 %shard_map.165 = (bf16[64,2048]{1,0:T(8,128)(2,1)S(1)}, bf16[64,2048]{1,0:T(8,128)(2,1)S(1)}, bf16[64,2048]{1,0:T(8,128)(2,1)S(1)}, bf16[64,2048]{1,0:T(8,128)(2...) custom-call(s32[8]{0:T(128)S(1)} %copy-done.13, ...), custom_call_target="tpu_custom_call" | custom-call | flops 4026531840 | bytes 15728640 | tf_op jit(solution)/shard_map/pallas_call | solution.py:546
  207.6 5.0 %collective-permute-done.43 = bf16[64,2048]{1,0:T(8,128)(2,1)S(1)} collective-permute-done((bf16[64,2048]{1,0:T(8,128)(2,1)S(1)}, bf16[64,2048]{1,0:T(8,128)(2,1)S(1)}, u32[]{:S(2)}, u32[]{:S(2)}) %collective-permute-start.43) | collective-permute-done | bytes 262176 | tf_op jit(solution)/shard_map/ppermute | solution.py:564
  213.1 14.3 %collective-permute-done.47 = bf16[64,2048]{1,0:T(8,128)(2,1)S(1)} collective-permute-done((bf16[64,2048]{1,0:T(8,128)(2,1)S(1)}, bf16[64,2048]{1,0:T(8,128)(2,1)S(1)}, u32[]{:S(2)}, u32[]{:S(2)}) %collective-permute-start.47) | collective-permute-done | bytes 262176 | tf_op jit(solution)/shard_map/ppermute | solution.py:564
  227.5 4.3 %collective-permute-start.48 = (bf16[64,2048]{1,0:T(8,128)(2,1)S(1)}, bf16[64,2048]{1,0:T(8,128)(2,1)S(1)}, u32[]{:S(2)}, u32[]{:S(2)}) collective-permute-start(bf16[64,2048]{1,0:T(8,128)(2,1)S(1)} %add_convert_fusion), channel_id=1, source_target_pairs={{0,3},{1,0},{2,1},{3,2},{4,7},{5,4},{6,5},{7,6},{8,11},{9,8},{10,9... | collective-permute-start | bytes 786440 | tf_op jit(solution)/shard_map/ppermute | solution.py:564
  238.4 4.3 %collective-permute-start.51 = (f32[8,128]{1,0:T(8,128)S(1)}, f32[8,128]{1,0:T(8,128)S(1)}, u32[]{:S(2)}, u32[]{:S(2)}) collective-permute-start(f32[8,128]{1,0:T(8,128)S(1)} %get-tuple-element.49), channel_id=1, source_target_pairs={{0,3},{1,2},{2,1},{3,0},{4,7},{5,6},{6,5},{7,4},{8,11},{9,10},{10,... | collective-permute-start | bytes 12296 | tf_op jit(solution)/shard_map/ppermute | solution.py:732
  (197 shorter events, 93.2 us)
Async XLA Ops:
  9.0 38.7 %collective-permute-start.7 = (bf16[6,256,256]{2,1,0:T(8,128)(2,1)S(1)}, bf16[6,256,256]{2,1,0:T(8,128)(2,1)S(1)}, u32[]{:S(2)}, u32[]{:S(2)}) collective-permute-start(bf16[6,256,256]{2,1,0:T(8,128)(2,1)S(1)} %shard_map.159.refs_8_), channel_id=1, source_target_pairs={{0,8},{4,12},{8,0},{12,4},{16,24},{20,28},{24,16},{28,20},{1,9},{5... | collective-permute-start | bytes 2359304 | tf_op jit(solution)/shard_map/ppermute | solution.py:568
  10.6 40.1 %collective-permute-start.9 = (bf16[6,256,256]{2,1,0:T(8,128)(2,1)S(1)}, bf16[6,256,256]{2,1,0:T(8,128)(2,1)}, u32[]{:S(2)}, u32[]{:S(2)}) collective-permute-start(bf16[6,256,256]{2,1,0:T(8,128)(2,1)S(1)} %shard_map.159.refs_8_), channel_id=1, source_target_pairs={{0,16},{4,20},{8,24},{12,28},{16,0},{20,4},{24,8},{28,12},{1,17},{... | collective-permute-start | bytes 2359304 | tf_op jit(solution)/shard_map/ppermute | solution.py:568
  32.8 32.8 %collective-permute-start.6 = (bf16[6,256,256]{2,1,0:T(8,128)(2,1)S(1)}, bf16[6,256,256]{2,1,0:T(8,128)(2,1)S(1)}, u32[]{:S(2)}, u32[]{:S(2)}) collective-permute-start(bf16[6,256,256]{2,1,0:T(8,128)(2,1)S(1)} %shard_map.159.refs_8_), channel_id=1, source_target_pairs={{0,4},{4,0},{8,12},{12,8},{16,20},{20,16},{24,28},{28,24},{1,5},{5... | collective-permute-start | bytes 2359304 | tf_op jit(solution)/shard_map/ppermute | solution.py:568
  35.0 16.8 %collective-permute-start.20 = (bf16[512,256]{1,0:T(8,128)(2,1)}, bf16[512,256]{1,0:T(8,128)(2,1)S(1)}, u32[]{:S(2)}, u32[]{:S(2)}) collective-permute-start(bf16[512,256]{1,0:T(8,128)(2,1)} %refs_0_.4), channel_id=1, source_target_pairs={{0,24},{4,28},{8,16},{12,20},{16,8},{20,12},{24,0},{28,4},{1,25},{... | collective-permute-start | bytes 786440 | tf_op jit(solution)/shard_map/ppermute | solution.py:568
  50.7 18.4 %collective-permute-start.8 = (bf16[6,256,256]{2,1,0:T(8,128)(2,1)S(1)}, bf16[6,256,256]{2,1,0:T(8,128)(2,1)}, u32[]{:S(2)}, u32[]{:S(2)}) collective-permute-start(bf16[6,256,256]{2,1,0:T(8,128)(2,1)S(1)} %collective-permute-done.7.refs_10_), channel_id=1, source_target_pairs={{0,4},{4,0},{8,12},{12,8},{16,20},{20,16},{24,28},{28,24},{1,5},{5... | collective-permute-start | bytes 2359304 | tf_op jit(solution)/shard_map/ppermute | solution.py:568
  66.5 49.9 %collective-permute-start.35 = (bf16[15,256,256]{2,1,0:T(8,128)(2,1)S(1)}, bf16[15,256,256]{2,1,0:T(8,128)(2,1)}, u32[]{:S(2)}, u32[]{:S(2)}) collective-permute-start(bf16[15,256,256]{2,1,0:T(8,128)(2,1)S(1)} %shard_map.163.refs_6_.refs_2_), channel_id=1, source_target_pairs={{0,16},{4,20},{8,24},{12,28},{16,0},{20,4},{24,8},{28,12},{1,17},{... | collective-permute-start | bytes 5898248 | tf_op jit(solution)/shard_map/ppermute | solution.py:568
  69.1 58.5 %collective-permute-start.33 = (bf16[15,256,256]{2,1,0:T(8,128)(2,1)S(1)}, bf16[15,256,256]{2,1,0:T(8,128)(2,1)S(1)}, u32[]{:S(2)}, u32[]{:S(2)}) collective-permute-start(bf16[15,256,256]{2,1,0:T(8,128)(2,1)S(1)} %shard_map.163.refs_6_.refs_2_), channel_id=1, source_target_pairs={{0,8},{4,12},{8,0},{12,4},{16,24},{20,28},{24,16},{28,20},{1,9},{5... | collective-permute-start | bytes 5898248 | tf_op jit(solution)/shard_map/ppermute | solution.py:568
  70.9 20.4 %collective-permute-start.17 = (bf16[512,256]{1,0:T(8,128)(2,1)}, bf16[512,256]{1,0:T(8,128)(2,1)S(1)}, u32[]{:S(2)}, u32[]{:S(2)}) collective-permute-start(bf16[512,256]{1,0:T(8,128)(2,1)} %copy-done.23), channel_id=1, source_target_pairs={{0,4},{4,0},{8,12},{12,8},{16,20},{20,16},{24,28},{28,24},{1,5},{5... | collective-permute-start | bytes 786440 | tf_op jit(solution)/shard_map/ppermute | solution.py:568
  70.9 20.3 %collective-permute-start.19 = (bf16[512,256]{1,0:T(8,128)(2,1)}, bf16[512,256]{1,0:T(8,128)(2,1)S(1)}, u32[]{:S(2)}, u32[]{:S(2)}) collective-permute-start(bf16[512,256]{1,0:T(8,128)(2,1)} %copy-done.27), channel_id=1, source_target_pairs={{0,4},{4,0},{8,12},{12,8},{16,20},{20,16},{24,28},{28,24},{1,5},{5... | collective-permute-start | bytes 786440 | tf_op jit(solution)/shard_map/ppermute | solution.py:568
  71.4 19.8 %collective-permute-start.21 = (bf16[512,256]{1,0:T(8,128)(2,1)}, bf16[512,256]{1,0:T(8,128)(2,1)S(1)}, u32[]{:S(2)}, u32[]{:S(2)}) collective-permute-start(bf16[512,256]{1,0:T(8,128)(2,1)} %copy-done.33), channel_id=1, source_target_pairs={{0,4},{4,0},{8,12},{12,8},{16,20},{20,16},{24,28},{28,24},{1,5},{5... | collective-permute-start | bytes 786440 | tf_op jit(solution)/shard_map/ppermute | solution.py:568
  94.0 39.5 %collective-permute-start.32 = (bf16[15,256,256]{2,1,0:T(8,128)(2,1)S(1)}, bf16[15,256,256]{2,1,0:T(8,128)(2,1)S(1)}, u32[]{:S(2)}, u32[]{:S(2)}) collective-permute-start(bf16[15,256,256]{2,1,0:T(8,128)(2,1)S(1)} %shard_map.163.refs_6_.refs_2_), channel_id=1, source_target_pairs={{0,4},{4,0},{8,12},{12,8},{16,20},{20,16},{24,28},{28,24},{1,5},{5... | collective-permute-start | bytes 5898248 | tf_op jit(solution)/shard_map/ppermute | solution.py:568
  94.5 16.2 %collective-permute-start.24 = (bf16[64,2048]{1,0:T(8,128)(2,1)S(1)}, bf16[64,2048]{1,0:T(8,128)(2,1)S(1)}, u32[]{:S(2)}, u32[]{:S(2)}) collective-permute-start(bf16[64,2048]{1,0:T(8,128)(2,1)S(1)} %get-tuple-element.34), channel_id=1, source_target_pairs={{0,1},{1,2},{2,3},{3,0},{4,5},{5,6},{6,7},{7,4},{8,9},{9,10},{10,1... | collective-permute-start | bytes 786440 | tf_op jit(solution)/shard_map/ppermute | solution.py:564
  116.4 16.2 %collective-permute-start.27 = (bf16[64,2048]{1,0:T(8,128)(2,1)S(1)}, bf16[64,2048]{1,0:T(8,128)(2,1)S(1)}, u32[]{:S(2)}, u32[]{:S(2)}) collective-permute-start(bf16[64,2048]{1,0:T(8,128)(2,1)S(1)} %add_convert_fusion.2), channel_id=1, source_target_pairs={{0,3},{1,0},{2,1},{3,2},{4,7},{5,4},{6,5},{7,6},{8,11},{9,8},{10,9... | collective-permute-start | bytes 786440 | tf_op jit(solution)/shard_map/ppermute | solution.py:564
  126.6 20.3 %collective-permute-start.37 = (bf16[8,256,256]{2,1,0:T(8,128)(2,1)S(1)}, bf16[8,256,256]{2,1,0:T(8,128)(2,1)S(1)}, u32[]{:S(2)}, u32[]{:S(2)}) collective-permute-start(bf16[8,256,256]{2,1,0:T(8,128)(2,1)S(1)} %slice.18), channel_id=1, source_target_pairs={{0,8},{4,12},{8,0},{12,4},{16,24},{20,28},{24,16},{28,20},{1,9},{5... | collective-permute-start | bytes 3145736 | tf_op jit(solution)/shard_map/ppermute | solution.py:568
  127.6 58.2 %collective-permute-start.34 = (bf16[15,256,256]{2,1,0:T(8,128)(2,1)S(1)}, bf16[15,256,256]{2,1,0:T(8,128)(2,1)S(1)}, u32[]{:S(2)}, u32[]{:S(2)}) collective-permute-start(bf16[15,256,256]{2,1,0:T(8,128)(2,1)S(1)} %collective-permute-done.33.refs_8_.refs_4_), channel_id=1, source_target_pairs={{0,4},{4,0},{8,12},{12,8},{16,20},{20,16},{24,28},{28,24},{1,5},{5... | collective-permute-start | bytes 5898248 | tf_op jit(solution)/shard_map/ppermute | solution.py:568
  127.6 58.2 %collective-permute-start.36 = (bf16[15,256,256]{2,1,0:T(8,128)(2,1)}, bf16[15,256,256]{2,1,0:T(8,128)(2,1)S(1)}, u32[]{:S(2)}, u32[]{:S(2)}) collective-permute-start(bf16[15,256,256]{2,1,0:T(8,128)(2,1)} %collective-permute-done.35.refs_10_.refs_6_), channel_id=1, source_target_pairs={{0,4},{4,0},{8,12},{12,8},{16,20},{20,16},{24,28},{28,24},{1,5},{5... | collective-permute-start | bytes 5898248 | tf_op jit(solution)/shard_map/ppermute | solution.py:568
  132.6 22.3 %collective-permute-start.38 = (bf16[7,256,256]{2,1,0:T(8,128)(2,1)S(1)}, bf16[7,256,256]{2,1,0:T(8,128)(2,1)S(1)}, u32[]{:S(2)}, u32[]{:S(2)}) collective-permute-start(bf16[7,256,256]{2,1,0:T(8,128)(2,1)S(1)} %slice.19), channel_id=1, source_target_pairs={{0,16},{4,20},{8,24},{12,28},{16,0},{20,4},{24,8},{28,12},{1,17},{... | collective-permute-start | bytes 2752520 | tf_op jit(solution)/shard_map/ppermute | solution.py:568
  133.5 21.4 %collective-permute-start.28 = (bf16[64,2048]{1,0:T(8,128)(2,1)S(1)}, bf16[64,2048]{1,0:T(8,128)(2,1)S(1)}, u32[]{:S(2)}, u32[]{:S(2)}) collective-permute-start(bf16[64,2048]{1,0:T(8,128)(2,1)S(1)} %get-tuple-element.39.refs_0_), channel_id=1, source_target_pairs={{0,1},{1,2},{2,3},{3,0},{4,5},{5,6},{6,7},{7,4},{8,9},{9,10},{10,1... | collective-permute-start | bytes 786440 | tf_op jit(solution)/shard_map/ppermute | solution.py:564
  146.9 38.9 %collective-permute-start.39 = (bf16[8,256,256]{2,1,0:T(8,128)(2,1)S(1)}, bf16[8,256,256]{2,1,0:T(8,128)(2,1)S(1)}, u32[]{:S(2)}, u32[]{:S(2)}) collective-permute-start(bf16[8,256,256]{2,1,0:T(8,128)(2,1)S(1)} %collective-permute-done.37.refs_12_.refs_8_), channel_id=1, source_target_pairs={{0,4},{4,0},{8,12},{12,8},{16,20},{20,16},{24,28},{28,24},{1,5},{5... | collective-permute-start | bytes 3145736 | tf_op jit(solution)/shard_map/ppermute | solution.py:568
  154.9 26.7 %collective-permute-start.40 = (bf16[7,256,256]{2,1,0:T(8,128)(2,1)S(1)}, bf16[7,256,256]{2,1,0:T(8,128)(2,1)S(1)}, u32[]{:S(2)}, u32[]{:S(2)}) collective-permute-start(bf16[7,256,256]{2,1,0:T(8,128)(2,1)S(1)} %collective-permute-done.38.refs_13_.refs_9_), channel_id=1, source_target_pairs={{0,4},{4,0},{8,12},{12,8},{16,20},{20,16},{24,28},{28,24},{1,5},{5... | collective-permute-start | bytes 2752520 | tf_op jit(solution)/shard_map/ppermute | solution.py:568
  203.8 28.0 %collective-permute-start.45 = (bf16[64,2048]{1,0:T(8,128)(2,1)S(1)}, bf16[64,2048]{1,0:T(8,128)(2,1)S(1)}, u32[]{:S(2)}, u32[]{:S(2)}) collective-permute-start(bf16[64,2048]{1,0:T(8,128)(2,1)S(1)} %get-tuple-element.44), channel_id=1, source_target_pairs={{0,1},{1,2},{2,3},{3,0},{4,5},{5,6},{6,7},{7,4},{8,9},{9,10},{10,1... | collective-permute-start | bytes 786440 | tf_op jit(solution)/shard_map/ppermute | solution.py:564
  204.4 27.4 %collective-permute-start.46 = (bf16[64,2048]{1,0:T(8,128)(2,1)S(1)}, bf16[64,2048]{1,0:T(8,128)(2,1)S(1)}, u32[]{:S(2)}, u32[]{:S(2)}) collective-permute-start(bf16[64,2048]{1,0:T(8,128)(2,1)S(1)} %get-tuple-element.45), channel_id=1, source_target_pairs={{0,3},{1,0},{2,1},{3,2},{4,7},{5,4},{6,5},{7,6},{8,11},{9,8},{10,9... | collective-permute-start | bytes 786440 | tf_op jit(solution)/shard_map/ppermute | solution.py:564
  207.6 19.8 %collective-permute-start.47 = (bf16[64,2048]{1,0:T(8,128)(2,1)S(1)}, bf16[64,2048]{1,0:T(8,128)(2,1)S(1)}, u32[]{:S(2)}, u32[]{:S(2)}) collective-permute-start(bf16[64,2048]{1,0:T(8,128)(2,1)S(1)} %get-tuple-element.47), channel_id=1, source_target_pairs={{0,3},{1,0},{2,1},{3,2},{4,7},{5,4},{6,5},{7,6},{8,11},{9,8},{10,9... | collective-permute-start | bytes 786440 | tf_op jit(solution)/shard_map/ppermute | solution.py:564
  212.7 22.2 %collective-permute-start.44 = (bf16[64,2048]{1,0:T(8,128)(2,1)S(1)}, bf16[64,2048]{1,0:T(8,128)(2,1)S(1)}, u32[]{:S(2)}, u32[]{:S(2)}) collective-permute-start(bf16[64,2048]{1,0:T(8,128)(2,1)S(1)} %add_convert_fusion.1), channel_id=1, source_target_pairs={{0,1},{1,2},{2,3},{3,0},{4,5},{5,6},{6,7},{7,4},{8,9},{9,10},{10,1... | collective-permute-start | bytes 786440 | tf_op jit(solution)/shard_map/ppermute | solution.py:564
  (74 other events, 919.9 us)
